TPU v7x, 8 devices: a whole 2x2x1 slice. The times are simulated.
8 devices in a mesh: data: 1 (over z), node: 2 (over y), expert: 4 (over x, core).
Axes of the slice: x: 2, y: 2, z: 1, core: 2. Of those that a mesh axis runs over, the one named last changes fastest.
Arguments:
- tokens: bfloat16 [2048, 2048], P(('data', 'node', 'expert'))
- expert_ids: int32 [2048, 8], P(('data', 'node', 'expert'))
- gate_weights: float32 [2048, 8], P(('data', 'node', 'expert'))
- slot_ids: int32 [2048, 8], P(('data', 'node', 'expert'))
- w_gate: bfloat16 [128, 2048, 768], P(('node', 'expert'))
- w_up: bfloat16 [128, 2048, 768], P(('node', 'expert'))
- w_down: bfloat16 [128, 768, 2048], P(('node', 'expert'))
Outputs:
- output: bfloat16 [2048, 2048], P(('data', 'node', 'expert'))
All inputs are finite; a program needn't handle non-finite values.
Results may differ from a plain program's by a relative error of at most 0.00154.
Values are sent between devices in bfloat16 or wider.
A program may use at most 1 GiB of HBM per device.

v0:
```python
import jax
import jax.numpy as jnp
from jax import lax
from jax.sharding import PartitionSpec as P

CAP_FACTOR = 2


def capacity(rows, top_k, experts):
    return ((CAP_FACTOR * rows * top_k + 8 * experts - 1) // (8 * experts)) * 8


def solution(mesh):
    group_axes = ("node", "expert")
    group_size = mesh.shape["node"] * mesh.shape["expert"]
    tok_spec = P(("data", "node", "expert"), None)
    weight_spec = P(("node", "expert"), None, None)

    def local_layer(tokens, expert_ids, gate_weights, slot_ids, w_gate, w_up, w_down):
        rows, width = tokens.shape
        top_k = expert_ids.shape[1]
        local_experts = w_gate.shape[0]
        experts = local_experts * group_size
        slot_count = capacity(rows, top_k, experts)
        flat_pos = jnp.where(slot_ids >= 0, expert_ids * slot_count + slot_ids, experts * slot_count)
        tok_index = jnp.broadcast_to(jnp.arange(rows, dtype=jnp.int32)[:, None], (rows, top_k))
        src_table = jnp.full((experts * slot_count,), rows, jnp.int32).at[flat_pos.reshape(-1)].set(tok_index.reshape(-1), mode="drop")
        send_buf = jnp.take(tokens, src_table, axis=0, mode="fill", fill_value=0)
        send_buf = send_buf.reshape(group_size, local_experts, 1, slot_count, width)
        recv_buf = lax.all_to_all(send_buf, group_axes, 0, 2, tiled=True)
        recv_buf = recv_buf.reshape(local_experts, group_size * slot_count, width)
        proj_gate = jnp.einsum("erd,edf->erf", recv_buf, w_gate, preferred_element_type=jnp.float32)
        proj_up = jnp.einsum("erd,edf->erf", recv_buf, w_up, preferred_element_type=jnp.float32)
        hidden = (jax.nn.silu(proj_gate) * proj_up).astype(jnp.bfloat16)
        expert_out = jnp.einsum("erf,efd->erd", hidden, w_down, preferred_element_type=jnp.float32).astype(jnp.bfloat16)
        expert_out = expert_out.reshape(local_experts, group_size, slot_count, width)
        returned = lax.all_to_all(expert_out, group_axes, 1, 0, tiled=True)
        returned = returned.reshape(experts * slot_count, width)
        picked = jnp.take(returned, flat_pos, axis=0, mode="fill", fill_value=0)
        combined = jnp.sum(gate_weights[:, :, None] * picked.astype(jnp.float32), axis=1)
        return combined.astype(jnp.bfloat16)

    return jax.shard_map(local_layer, mesh=mesh, in_specs=(tok_spec, tok_spec, tok_spec, tok_spec, weight_spec, weight_spec, weight_spec), out_specs=tok_spec, check_vma=False)
```

profile of v0, /device:TPU:0, one launch (start us, length us, event | category | flops | bytes accessed | tf_op | source)
XLA Modules:
  0.0 547.2 jit_solution(9256766711455393232)
XLA Ops:
  0.0 0.0 copy-start
  0.0 1.4 compare_and_fusion.1
  1.4 0.1 copy.21
  1.5 0.1 reshape.74
  1.7 0.1 reshape.99
  1.8 8.1 %scatter_custom_fusion = s32[4096]{0:T(1024)S(1)} fusion(s32[2048]{0:T(1024)S(1)} %bitcast.33, s32[2048]{0:T(1024)S(1)} %reshape.99, s32[]{:T(128)} %constant.24.clone.1), kind=kCustom, calls=%fused_computation.15 | custom fusion | bytes 16388 | tf_op jit(solution)/shard_map/scatter | solution.py:27
  9.9 0.1 broadcast_in_dim.45
  10.0 0.0 copy-done
  10.0 20.9 %gather_fusion = bf16[4096,2048]{1,0:T(8,128)(2,1)} fusion(bf16[256,2048]{1,0:T(8,128)(2,1)S(1)} %copy-done, s32[4096]{0:T(1024)S(1)} %fusion.3), kind=kCustom, calls=%fused_computation | custom fusion | bytes 33570816 | tf_op jit(solution)/shard_map/jit(_take)/gather | solution.py:28
  30.9 0.0 copy-done.2
  30.9 8.3 %broadcast_select_fusion = bf16[8,16,1,32,2048]{4,3,1,2,0:T(8,128)(2,1)S(1)} fusion(bf16[8,16,1,32,2048]{4,3,1,2,0:T(8,128)(2,1)} %bitcast.28, pred[8,16,32]{2,1,0:T(8,128)(4,1)S(1)} %broadcast_in_dim.45), kind=kLoop, calls=%fused_computation.4 | loop fusion | flops 8388608 | bytes 33558528 | tf_op jit(solution)/shard_map/jit(_take)/select_n | solution.py:28
  39.2 188.0 %all_to_all.30 = bf16[8,16,1,32,2048]{4,3,1,2,0:T(8,128)(2,1)S(1)} all-to-all(bf16[8,16,1,32,2048]{4,3,1,2,0:T(8,128)(2,1)S(1)} %broadcast_select_fusion), channel_id=1, replica_groups=mesh['data'=1,'node'=2,'expert'=4] {'node','expert'}, dimensions={0} | all-to-all | bytes 33554432 | tf_op jit(solution)/shard_map/all_to_all | solution.py:30
  227.1 6.5 %copy.23 = bf16[1,16,8,1,32,2048]{5,4,2,1,3,0:T(8,128)(2,1)} copy(bf16[1,16,8,1,32,2048]{5,4,1,2,3,0:T(8,128)(2,1)S(1)} %bitcast.29) | data formatting | bytes 33554432 | tf_op jit(solution)/shard_map/all_to_all | solution.py:30
  233.6 28.5 %fusion.7 = f32[16,256,768]{2,1,0:T(8,128)} fusion(bf16[16,256,2048]{2,1,0:T(8,128)(2,1)} %bitcast.30, bf16[16,2048,768]{2,1,0:T(8,128)(2,1)} %param.11), kind=kOutput, calls=%fused_computation.21 | convolution fusion | flops 12884901888 | bytes 79691776 | tf_op jit(solution)/shard_map/erd,edf->erf/dot_general | solution.py:32
  262.1 47.7 %convolution_convert_fusion = bf16[16,256,2048]{2,1,0:T(8,128)(2,1)} fusion(bf16[16,768,2048]{2,1,0:T(8,128)(2,1)} %param.13, f32[16,256,768]{2,1,0:T(8,128)} %fusion.7, bf16[16,256,2048]{2,1,0:T(8,128)(2,1)} %bitcast.31, bf16[16,2048,768]{2,1,0:T(8,128)(2,1)} %param.12), kind=kOutput, calls=%fused_computation.5 | convolution fusion | flops 25797066752 | bytes 146800640 | tf_op jit(solution)/shard_map/erf,efd->erd/dot_general | solution.py:35
  309.8 14.1 %copy.24 = bf16[16,8,32,2048]{3,2,0,1:T(8,128)(2,1)} copy(bf16[16,8,32,2048]{3,2,1,0:T(8,128)(2,1)} %bitcast.32) | data formatting | bytes 33554432 | tf_op jit(solution)/shard_map/reshape | solution.py:36
  323.9 4.8 all-to-all-start.1
  328.7 0.1 copy.25
  328.9 0.1 reshape.89
  329.0 0.2 copy.20
  329.2 0.1 copy.19
  329.3 183.2 %all-to-all-done.1 = bf16[16,8,32,2048]{3,2,0,1:T(8,128)(2,1)} async-done(((bf16[16,8,32,2048]{3,2,0,1:T(8,128)(2,1)}), bf16[16,8,32,2048]{3,2,0,1:T(8,128)(2,1)}, u32[]{:S(2)}, u32[]{:S(2)}) %all-to-all-start.1) | async-done | bytes 16777248 | tf_op jit(solution)/shard_map/all_to_all | solution.py:37
  512.5 24.4 %gather_fusion.1 = bf16[2048,2048]{1,0:T(8,128)(2,1)} fusion(bf16[4096,2048]{1,0:T(8,128)(2,1)} %bitcast.9, s32[2048]{0:T(1024)S(1)} %broadcast_clamp_fusion), kind=kCustom, calls=%fused_computation.1 | custom fusion | bytes 16785408 | tf_op jit(solution)/shard_map/jit(_take)/gather | solution.py:39
  536.9 10.3 %multiply_reduce_fusion = bf16[256,2048]{1,0:T(8,128)(2,1)} fusion(bf16[2048,2048]{1,0:T(8,128)(2,1)} %gather_fusion.1, f32[256,8]{1,0:T(8,128)S(1)} %copy.19, pred[256,8]{1,0:T(8,128)(4,1)S(1)} %copy.20), kind=kLoop, calls=%fused_computation.3 | loop fusion | flops 16252928 | bytes 9447424 | tf_op jit(solution)/shard_map/reduce_sum | solution.py:40
  (15 shorter events, 0.1 us)
Async XLA Ops:
  0.0 10.0 %copy-start = (bf16[256,2048]{1,0:T(8,128)(2,1)S(1)}, bf16[256,2048]{1,0:T(8,128)(2,1)}, u32[]{:S(2)}) copy-start(bf16[256,2048]{1,0:T(8,128)(2,1)} %param.7) | copy-start | bytes 3145732
  1.4 29.5 %copy-start.2 = (s32[256,8]{0,1:T(8,128)}, s32[256,8]{0,1:T(8,128)S(1)}, u32[]{:S(2)}) copy-start(s32[256,8]{0,1:T(8,128)S(1)} %get-tuple-element.6) | copy-start | bytes 24580
  323.9 4.8 copy-start.3
  323.9 5.1 copy-start.5
  323.9 5.2 copy-start.4
  323.9 188.6 %all-to-all-start.1 = ((bf16[16,8,32,2048]{3,2,0,1:T(8,128)(2,1)}), bf16[16,8,32,2048]{3,2,0,1:T(8,128)(2,1)}, u32[]{:S(2)}, u32[]{:S(2)}) async-start(bf16[16,8,32,2048]{3,2,0,1:T(8,128)(2,1)} %copy.24), calls=%async_computation.1 | async-start | bytes 33554432 | tf_op jit(solution)/shard_map/all_to_all | solution.py:37
  512.5 34.7 %copy-start.1 = (bf16[256,2048]{1,0:T(8,128)(2,1)S(1)}, bf16[256,2048]{1,0:T(8,128)(2,1)}, u32[]{:S(2)}) copy-start(bf16[256,2048]{1,0:T(8,128)(2,1)} %param.7) | copy-start | bytes 3145732
where the time goes:
time: 548 us; the launch traced here: 547 us
  blocking collectives  188 us (34%)
  waiting for transfers between devices  183 us (33%)
  matrix products  76.2 us (14%)
  local copies, waits for them, and re-layouts  74.9 us (14%)
  other arithmetic  20.1 us (4%)
    all_to_all x1, blocking collectives, local_layer(): recv_buf = lax.all_to_all(send_buf, group_axes, 0, 2, tiled=True)  188 us
    all_to_all x1, waiting for transfers between devices, local_layer(): returned = lax.all_to_all(expert_out, group_axes, 1, 0, tiled=True)  183 us
    dot_general x1, matrix products, local_layer(): jnp.einsum('erf,efd->erd', hidden, w_down, preferred_element_type=jnp.flo...  47.7 us
    dot_general x1, matrix products, local_layer(): jnp.einsum('erd,edf->erf', recv_buf, w_gate, preferred_element_type=jnp.f...  28.5 us
    gather x1, local copies, waits for them, and re-layouts, local_layer(): picked = jnp.take(returned, flat_pos, axis=0, mode='fill', fill_value=0)  24.4 us
    gather x1, local copies, waits for them, and re-layouts, local_layer(): send_buf = jnp.take(tokens, src_table, axis=0, mode='fill', fill_value=0)  20.9 us
    reshape x1, local copies, waits for them, and re-layouts, local_layer(): expert_out.reshape(local_experts, group_size, slot_count, width)  14.1 us
  transfers between devices with their start and end apart: 1, of which 1 were waited for; matrix products, arithmetic and copies ran while one was open for 0% of the time, Pallas kernels for 0%

commit v1 on v0

v1 whole, which is shorter than its diff:
```python
import functools

import jax
import jax.numpy as jnp
from jax import lax
from jax.experimental import pallas as pl
from jax.experimental.pallas import tpu as pltpu
from jax.sharding import PartitionSpec as P

CAP_FACTOR = 2
MESH = pl.DeviceIdType.MESH
F32 = jnp.float32
BF16 = jnp.bfloat16

ROWS = 256
WIDTH = 2048
FF = 768
LOCAL = 16
CAP = 32
GROUP = 8
SLOTS = LOCAL * CAP
KC = 512
NK = WIDTH // KC
NB = 4
CC = 256
NC = WIDTH // CC
NBD = 8
LAG = 2

OWN = 0
PBUF = 64
DRECV = 80
RA1 = 144
RB1 = 160
RA2 = 176
RB2 = 184
NBLK = 192


def capacity(rows, top_k, experts):
    return ((CAP_FACTOR * rows * top_k + 8 * experts - 1) // (8 * experts)) * 8


def layer_kernel(
    r_ref, tok_ref, wg_ref, wu_ref, wd_ref, out_ref,
    rall, rt, xall, pmat, gbuf, big, wbuf, hbuf, dbuf, ybuf,
    lsem, rs_sem, rr_sem, xs_sem, xr_sem, w_sem, d_sem,
    ds_sem, dr_sem, is_sem, ir_sem, ready,
):
    data = lax.axis_index("data")
    y = lax.axis_index("node")
    ex = lax.axis_index("expert")
    x = ex // 2
    q = ex % 2
    g = y * 4 + ex
    flip = 1 - 2 * q
    gx = y * 4 + (1 - x) * 2 + q
    gy = (1 - y) * 4 + x * 2 + q
    gd = (1 - y) * 4 + (1 - x) * 2 + q
    gp = g + flip
    partner = (data, y, ex + flip)
    xn = (data, y, (1 - x) * 2 + q)
    yn = (data, 1 - y, ex)

    barrier = pltpu.get_barrier_semaphore()
    for d in range(1, GROUP):
        t = (g + d) % GROUP
        pl.semaphore_signal(barrier, inc=1, device_id=(data, t // 4, t % 4), device_id_type=MESH)

    def own_load(k):
        return pltpu.make_async_copy(
            tok_ref.at[:, pl.ds(k * KC, KC)],
            xall.at[pl.ds(pl.multiple_of((k * GROUP + g) * ROWS, ROWS), ROWS), :],
            lsem.at[k],
        )

    for k in range(NK):
        own_load(k).start()

    def w_load(i):
        k, e, slot = i // LOCAL, i % LOCAL, i % NB
        rows = pl.ds(pl.multiple_of(k * KC, KC), KC)
        return [
            pltpu.make_async_copy(ref.at[e, rows, :], wbuf.at[slot, j], w_sem.at[slot, j])
            for j, ref in enumerate((wg_ref, wu_ref))
        ]

    def d_load(i):
        c, e, slot = i // LOCAL, i % LOCAL, i % NBD
        cols = pl.ds(pl.multiple_of(c * CC, CC), CC)
        return pltpu.make_async_copy(wd_ref.at[e, :, cols], dbuf.at[slot], d_sem.at[slot])

    for i in range(NB):
        for cp in w_load(i):
            cp.start()
    for i in range(NBD):
        d_load(i).start()

    rall[pl.ds(pl.multiple_of(g * 16, 16), 16), :] = r_ref[...]
    pl.semaphore_wait(barrier, GROUP - 1)

    def r_copy(d, owner, dst):
        return pltpu.make_async_remote_copy(
            src_ref=r_ref,
            dst_ref=rall.at[pl.ds(pl.multiple_of(owner * 16, 16), 16), :],
            send_sem=rs_sem.at[d - 1],
            recv_sem=rr_sem.at[d - 1],
            device_id=(data, dst // 4, dst % 4),
            device_id_type=MESH,
        )

    for d in range(1, GROUP):
        r_copy(d, g, (g + d) % GROUP).start()

    def x_copy(i, k, s, dev, lo=0, n=ROWS):
        ref = xall.at[pl.ds(pl.multiple_of((k * GROUP + s) * ROWS + lo, 128), n), :]
        return pltpu.make_async_remote_copy(
            src_ref=ref, dst_ref=ref, send_sem=xs_sem.at[i, k], recv_sem=xr_sem.at[i, k],
            device_id=dev, device_id_type=MESH,
        )

    HALF = ROWS // 2

    def send(i, k):
        return x_copy(i, k, *(
            (g, partner),
            (g, xn),
            (g, yn),
            (gx, yn, 0, HALF),
            (gx, partner),
            (gy, xn, HALF, HALF),
            (gy, partner),
            (gd, partner),
        )[i])

    def arrival(i, k):
        return x_copy(i, k, *(
            (gp, partner),
            (gx, xn),
            (gy, yn),
            (gd, yn, 0, HALF),
            (gx + flip, partner),
            (gd, xn, HALF, HALF),
            (gy + flip, partner),
            (gd + flip, partner),
        )[i])

    def own(k):
        own_load(k).wait()
        for i in (1, 2, 0):
            send(i, k).start()

    def forward(k):
        arrival(1, k).wait_recv()
        send(3, k).start()
        send(4, k).start()
        arrival(2, k).wait_recv()
        send(5, k).start()
        send(6, k).start()

    def finish(k):
        arrival(3, k).wait_recv()
        arrival(5, k).wait_recv()
        send(7, k).start()
        for i in (0, 4, 6, 7):
            arrival(i, k).wait_recv()

    own(0)

    for d in range(1, GROUP):
        r_copy(d, (g + GROUP - d) % GROUP, g).wait_recv()
    rt[...] = jnp.transpose(rall[...])

    base = (g * SLOTS).astype(F32)
    PB = 64

    def build_p(i, carry):
        s, b = i // (SLOTS // PB), i % (SLOTS // PB)
        want = lax.broadcasted_iota(jnp.int32, (PB, ROWS), 0).astype(F32) + (base + (b * PB).astype(F32))
        pos = rall[pl.ds(pl.multiple_of(s * 16, 16), 8), :]
        hit = jnp.zeros((PB, ROWS), F32)
        for j in range(8):
            hit = jnp.where(pos[j : j + 1, :] == want, 1.0, hit)
        pmat[pl.ds(pl.multiple_of(i * PB, PB), PB), :] = hit.astype(BF16)
        return carry

    lax.fori_loop(0, GROUP * SLOTS // PB, build_p, 0)

    forward(0)
    own(1)
    finish(0)

    def build_g(i):
        s, half = i % GROUP, i // GROUP
        t0 = pl.multiple_of(half * 128, 128)
        v = pltpu.roll(rt[pl.ds(t0, 128), :], (128 - s * 16) % 128, 1)
        want = lax.broadcasted_iota(jnp.int32, (128, SLOTS), 1).astype(F32) + base
        sel = jnp.zeros((128, SLOTS), F32)
        for j in range(8):
            sel = jnp.where(v[:, j : j + 1] == want, v[:, 8 + j : 9 + j], sel)
        g1 = (sel * (1.0 - 2.0**-8)).astype(BF16)
        rest = sel - g1.astype(F32)
        g2 = rest.astype(BF16)
        g3 = (rest - g2.astype(F32)).astype(BF16)
        for p, part in enumerate((g1, g2, g3)):
            xall[pl.ds(pl.multiple_of(s * 768 + p * 256 + t0, 128), 128), :] = part

    def gather_rows(k):
        def body(i, carry):
            s, m = i // 2, i % 2
            pm = pmat[pl.ds(pl.multiple_of(i * 256, 256), 256), :]
            xs = xall[pl.ds(pl.multiple_of((k * GROUP + s) * ROWS, ROWS), ROWS), :]
            got = jnp.dot(pm, xs, preferred_element_type=F32).astype(BF16)
            gbuf[s, pl.ds(pl.multiple_of(m * 256, 256), 256), :] = got
            return carry

        lax.fori_loop(0, 2 * GROUP, body, 0)

    def block(i, n=1):
        return pl.ds(pl.multiple_of(i * 256, 256), n * 256)

    def experts(k, lo, hi):
        def body(e, carry):
            i = k * LOCAL + e
            slot = i % NB
            for cp in w_load(i):
                cp.wait()
            lhs = gbuf[:, pl.ds(pl.multiple_of(e * CAP, CAP), CAP), :].reshape(GROUP * CAP, KC)
            for n in range(FF // 256):
                vals = []
                for j in range(2):
                    v = jnp.dot(lhs, wbuf[slot, j, :, n * 256 : (n + 1) * 256], preferred_element_type=F32)
                    at = e * 12 + j * 6 + n * 2
                    if k > 0:
                        v = v + jnp.concatenate([big[block(at), :], big[block(at + 1), :]], axis=1)
                    if k < NK - 1:
                        big[block(at), :] = v[:, :128]
                        big[block(at + 1), :] = v[:, 128:]
                    vals.append(v)
                if k == NK - 1:
                    hbuf[e, :, n * 256 : (n + 1) * 256] = (jax.nn.silu(vals[0]) * vals[1]).astype(BF16)
            if k == NK - 1:
                build_g(e)

            @pl.when(i + NB < NK * LOCAL)
            def _():
                for cp in w_load(i + NB):
                    cp.start()

            return carry

        lax.fori_loop(lo, hi, body, 0)

    for k in range(NK):
        if k == NK - 1:
            for kk in range(NK - 1):
                for i in range(8):
                    send(i, kk).wait_send()
        gather_rows(k)
        experts(k, 0, 8)
        if k < NK - 1:
            forward(k + 1)
        if k < NK - 2:
            own(k + 2)
        experts(k, 8, LOCAL)
        if k < NK - 1:
            finish(k + 1)

    for dev in (partner, xn, yn):
        pl.semaphore_signal(ready, inc=1, device_id=dev, device_id_type=MESH)

    def part(core, d, to):
        dx, dy = d % 2, d // 2
        s = ((y + dy) % 2) * 4 + ((x + dx) % 2) * 2 + core
        ys = ybuf[s]
        gs = xall[pl.ds(pl.multiple_of(s * 768, 256), 768), :]
        v = jnp.dot(gs, ys, preferred_element_type=F32)
        v = v[0:256] + (v[256:512] + v[512:768])
        big[block(to + dx * 2 + dy), :] = v[:, :128]
        big[block(to + 4 + dy * 2 + dx), :] = v[:, 128:]

    def d2d(c):
        return pltpu.make_async_remote_copy(
            src_ref=big.at[block(PBUF + (c % 2) * 8, 8), :],
            dst_ref=big.at[block(DRECV + c * 8, 8), :],
            send_sem=ds_sem.at[c], recv_sem=dr_sem.at[c],
            device_id=partner, device_id_type=MESH,
        )

    def ici(i, c):
        src, dst, n, dev = (
            (OWN + c * 8 + 2, RA1 + c * 2, 2, xn),
            (OWN + c * 8 + 6, RB1 + c * 2, 2, yn),
            (OWN + c * 8 + 1, RA2 + c, 1, yn),
            (OWN + c * 8 + 5, RB2 + c, 1, xn),
        )[i]
        return pltpu.make_async_remote_copy(
            src_ref=big.at[block(src, n), :], dst_ref=big.at[block(dst, n), :],
            send_sem=is_sem.at[i, c], recv_sem=ir_sem.at[i, c],
            device_id=dev, device_id_type=MESH,
        )

    def second_hop(c):
        ici(0, c).wait_recv()
        big[block(OWN + c * 8 + 1), :] = big[block(OWN + c * 8 + 1), :] + big[block(RA1 + c * 2 + 1), :]
        ici(2, c).start()
        ici(1, c).wait_recv()
        big[block(OWN + c * 8 + 5), :] = big[block(OWN + c * 8 + 5), :] + big[block(RB1 + c * 2 + 1), :]
        ici(3, c).start()

    def column_chunk(c, carry):
        def down(e, inner):
            i = c * LOCAL + e
            d_load(i).wait()
            v = jnp.dot(hbuf[e], dbuf[i % NBD], preferred_element_type=F32).astype(BF16)
            ybuf[:, pl.ds(pl.multiple_of(e * CAP, CAP), CAP), :] = v.reshape(GROUP, CAP, CC)

            @pl.when(i + NBD < NC * LOCAL)
            def _():
                d_load(i + NBD).start()

            return inner

        lax.fori_loop(0, LOCAL, down, 0)

        @pl.when(c >= 2)
        def _():
            d2d(c - 2).wait_send()

        def theirs(d, inner):
            part(1 - q, d, PBUF + (c % 2) * 8)
            return inner

        lax.fori_loop(0, 4, theirs, 0)

        @pl.when(c == 0)
        def _():
            pl.semaphore_wait(ready, 3)

        d2d(c).start()

        def ours(d, inner):
            part(q, d, OWN + c * 8)
            return inner

        lax.fori_loop(0, 4, ours, 0)

        @pl.when(c >= LAG)
        def _():
            second_hop(c - LAG)

        d2d(c).wait_recv()

        def add(b, inner):
            big[block(OWN + c * 8 + b), :] = big[block(OWN + c * 8 + b), :] + big[block(DRECV + c * 8 + b), :]
            return inner

        lax.fori_loop(0, 8, add, 0)
        ici(0, c).start()
        ici(1, c).start()
        return carry

    lax.fori_loop(0, NC, column_chunk, 0)

    def tail(c, carry):
        second_hop(c)
        return carry

    lax.fori_loop(NC - LAG, NC, tail, 0)

    def final(c, carry):
        ici(2, c).wait_recv()
        a = big[block(OWN + c * 8), :] + big[block(RA1 + c * 2), :] + big[block(RA2 + c), :]
        ici(3, c).wait_recv()
        b = big[block(OWN + c * 8 + 4), :] + big[block(RB1 + c * 2), :] + big[block(RB2 + c), :]
        out_ref[:, pl.ds(pl.multiple_of(c * CC, CC), 128)] = a.astype(BF16)
        out_ref[:, pl.ds(pl.multiple_of(c * CC + 128, 128), 128)] = b.astype(BF16)
        for i in range(4):
            ici(i, c).wait_send()
        return carry

    lax.fori_loop(0, NC, final, 0)

    for c in (NC - 2, NC - 1):
        d2d(c).wait_send()
    for i in range(8):
        send(i, NK - 1).wait_send()
    for d in range(1, GROUP):
        r_copy(d, g, (g + d) % GROUP).wait_send()


def solution(mesh):
    group_axes = ("node", "expert")
    group_size = mesh.shape["node"] * mesh.shape["expert"]
    tok_spec = P(("data", "node", "expert"), None)
    weight_spec = P(("node", "expert"), None, None)

    def local_layer(tokens, expert_ids, gate_weights, slot_ids, w_gate, w_up, w_down):
        rows, width = tokens.shape
        top_k = expert_ids.shape[1]
        local_experts = w_gate.shape[0]
        slot_count = capacity(rows, top_k, local_experts * group_size)
        assert (rows, width, local_experts, slot_count, group_size) == (ROWS, WIDTH, LOCAL, CAP, GROUP)
        flat_pos = jnp.where(slot_ids >= 0, expert_ids * slot_count + slot_ids, -1)
        routing = jnp.concatenate([flat_pos.astype(F32), gate_weights], axis=1).T

        vmem = pl.BlockSpec(memory_space=pltpu.VMEM)
        hbm = pl.BlockSpec(memory_space=pl.ANY)
        dma = pltpu.SemaphoreType.DMA
        return pl.pallas_call(
            layer_kernel,
            out_shape=jax.ShapeDtypeStruct((rows, width), BF16),
            in_specs=[vmem, hbm, hbm, hbm, hbm],
            out_specs=vmem,
            scratch_shapes=[
                pltpu.VMEM((GROUP * 16, ROWS), F32),
                pltpu.VMEM((ROWS, GROUP * 16), F32),
                pltpu.VMEM((NK * GROUP * ROWS, KC), BF16),
                pltpu.VMEM((GROUP * SLOTS, ROWS), BF16),
                pltpu.VMEM((GROUP, SLOTS, KC), BF16),
                pltpu.VMEM((NBLK * 256, 128), F32),
                pltpu.VMEM((NB, 2, KC, FF), BF16),
                pltpu.VMEM((LOCAL, GROUP * CAP, FF), BF16),
                pltpu.VMEM((NBD, FF, CC), BF16),
                pltpu.VMEM((GROUP, SLOTS, CC), BF16),
                dma((NK,)),
                dma((GROUP - 1,)),
                dma((GROUP - 1,)),
                dma((8, NK)),
                dma((8, NK)),
                dma((NB, 2)),
                dma((NBD,)),
                dma((NC,)),
                dma((NC,)),
                dma((4, NC)),
                dma((4, NC)),
                pltpu.SemaphoreType.REGULAR,
            ],
            compiler_params=pltpu.CompilerParams(
                collective_id=0, has_side_effects=True, vmem_limit_bytes=67043328,
            ),
            cost_estimate=pl.CostEstimate(
                flops=6 * LOCAL * GROUP * CAP * WIDTH * FF,
                bytes_accessed=6 * LOCAL * WIDTH * FF,
                transcendentals=LOCAL * GROUP * CAP * FF,
            ),
            name="moe_layer",
        )(routing, tokens, w_gate, w_up, w_down)

    return jax.shard_map(local_layer, mesh=mesh, in_specs=(tok_spec, tok_spec, tok_spec, tok_spec, weight_spec, weight_spec, weight_spec), out_specs=tok_spec, check_vma=False)
```

time: 548 us -> 168 us (0.31)
  blocking collectives: 188 us -> 0 us
  waiting for transfers between devices: 183 us -> 0 us
  Pallas kernels: 0 us -> 164 us
  matrix products: 76.2 us -> 0 us
  local copies, waits for them, and re-layouts: 74.9 us -> 2.3 us
  other arithmetic: 20.1 us -> 2.02 us
    all_to_all x1 -> x0, blocking collectives: 188 us -> none  [local_layer(): recv_buf = lax.all_to_all(send_buf, group_axes, 0, 2, tiled=True)]
    all_to_all x1 -> x0, waiting for transfers between devices: 183 us -> none  [local_layer(): returned = lax.all_to_all(expert_out, group_axes, 1, 0, tiled=True)]
    pallas_call x0 -> x1, Pallas kernels: none -> 164 us  [local_layer(): pl.pallas_call(layer_kernel, out_shape=jax.ShapeDtypeStruct((rows, width)...]
    dot_general x2 -> x0, matrix products: 76.2 us -> none  [the longest x1 47.7 us: local_layer(): jnp.einsum('erf,efd->erd', hidden, w_down, preferred_element_type=jnp.flo...]
    gather x2 -> x0, local copies, waits for them, and re-layouts: 45.2 us -> none  [the longest x1 24.4 us: local_layer(): picked = jnp.take(returned, flat_pos, axis=0, mode='fill', fill_value=0)]
    reshape x3 -> x0, local copies, waits for them, and re-layouts: 14.3 us -> none  [the longest x1 14.1 us: local_layer(): expert_out.reshape(local_experts, group_size, slot_count, width)]
    reduce_sum x1 -> x0, other arithmetic: 10.3 us -> none  [local_layer(): jnp.sum(gate_weights[:, :, None] * picked.astype(jnp.float32), axis=1)]
    select_n x3 -> x0, other arithmetic: 8.29 us -> none  [the longest x1 8.27 us: local_layer(): send_buf = jnp.take(tokens, src_table, axis=0, mode='fill', fill_value=0)]
  transfers between devices with their start and end apart: 1 -> 0, of which waited for: 1 -> 0; matrix products, arithmetic and copies ran while one was open for 0% -> 0% of each run, Pallas kernels for 0% -> 0%
where the time goes in v1:
time: 168 us
  Pallas kernels  164 us (98%)
  local copies, waits for them, and re-layouts  2.3 us (1%)
  other arithmetic  2.02 us (1%)
    pallas_call x1, Pallas kernels, local_layer(): pl.pallas_call(layer_kernel, out_shape=jax.ShapeDtypeStruct((rows, width)...  164 us

profile of v1, /device:TPU:0, one launch (start us, length us, event | category | flops | bytes accessed | tf_op | source)
XLA Modules:
  0.0 168.0 jit_solution(3319717220769309924)
XLA Ops:
  0.0 0.7 select_convert_fusion
  0.7 1.3 maximum_bitcast_fusion.r_ref
  2.0 163.7 %moe_layer.1 = bf16[256,2048]{1,0:T(8,128)(2,1)} custom-call(f32[16,256]{1,0:T(8,128)} %maximum_bitcast_fusion.r_ref, bf16[256,2048]{1,0:T(8,128)(2,1)} %tok_ref.1, bf16[16,2048,768]{2,1,0:T(8,128)(2,1)} %wg_ref.1, bf16[16,2048,768]{2,1,0:T(8,128)(2,1)} %wu_ref.1, bf16[16,768,2048]{2,1,0:T(8,128)(2,1)} %wd_ref.1), custom_call_target="tpu_custom_call" | custom-call | flops 38654705664 | bytes 150994944 | tf_op jit(solution)/shard_map/moe_layer/pallas_call | solution.py:410
  165.7 2.3 %copy.9 = bf16[256,2048]{1,0:T(8,128)(2,1)} copy(bf16[256,2048]{1,0:T(8,128)(2,1)} %moe_layer.1) | data formatting | bytes 2097152

commit v2 on v1

--- a/solution.py
+++ b/solution.py
@@ -1,5 +1,3 @@
-import functools
-
 import jax
 import jax.numpy as jnp
 from jax import lax
@@ -19,9 +17,9 @@
 CAP = 32
 GROUP = 8
 SLOTS = LOCAL * CAP
-KC = 512
+KC = 256
 NK = WIDTH // KC
-NB = 4
+NB = 10
 CC = 256
 NC = WIDTH // CC
 NBD = 8
@@ -42,8 +40,8 @@
 
 
 def layer_kernel(
-    r_ref, tok_ref, wg_ref, wu_ref, wd_ref, out_ref,
-    rall, rt, xall, pmat, gbuf, big, wbuf, hbuf, dbuf, ybuf,
+    id_ref, slot_ref, gate_ref, tok_ref, wg_ref, wu_ref, wd_ref, out_ref,
+    rall, rt, xall, pmat, gmat, gbuf, big, wbuf, hbuf, dbuf,
     lsem, rs_sem, rr_sem, xs_sem, xr_sem, w_sem, d_sem,
     ds_sem, dr_sem, is_sem, ir_sem, ready,
 ):
@@ -96,13 +94,17 @@
     for i in range(NBD):
         d_load(i).start()
 
-    rall[pl.ds(pl.multiple_of(g * 16, 16), 16), :] = r_ref[...]
+    mine = pl.multiple_of(g * 16, 16)
+    flat_pos = jnp.where(slot_ref[...] >= 0, id_ref[...] * CAP + slot_ref[...], -1)
+    rall[pl.ds(mine, 8), :] = flat_pos.astype(F32)
+    rall[pl.ds(mine + 8, 8), :] = gate_ref[...]
     pl.semaphore_wait(barrier, GROUP - 1)
 
     def r_copy(d, owner, dst):
+        ref = rall.at[pl.ds(pl.multiple_of(owner * 16, 16), 16), :]
         return pltpu.make_async_remote_copy(
-            src_ref=r_ref,
-            dst_ref=rall.at[pl.ds(pl.multiple_of(owner * 16, 16), 16), :],
+            src_ref=ref,
+            dst_ref=ref,
             send_sem=rs_sem.at[d - 1],
             recv_sem=rr_sem.at[d - 1],
             device_id=(data, dst // 4, dst % 4),
@@ -166,13 +168,16 @@
             arrival(i, k).wait_recv()
 
     own(0)
+    own(1)
 
     for d in range(1, GROUP):
         r_copy(d, (g + GROUP - d) % GROUP, g).wait_recv()
     rt[...] = jnp.transpose(rall[...])
 
     base = (g * SLOTS).astype(F32)
+    ybuf = pmat
     PB = 64
+    GB = 64
 
     def build_p(i, carry):
         s, b = i // (SLOTS // PB), i % (SLOTS // PB)
@@ -181,21 +186,15 @@
         hit = jnp.zeros((PB, ROWS), F32)
         for j in range(8):
             hit = jnp.where(pos[j : j + 1, :] == want, 1.0, hit)
-        pmat[pl.ds(pl.multiple_of(i * PB, PB), PB), :] = hit.astype(BF16)
+        pmat[s, pl.ds(pl.multiple_of(b * PB, PB), PB), :] = hit.astype(BF16)
         return carry
 
-    lax.fori_loop(0, GROUP * SLOTS // PB, build_p, 0)
-
-    forward(0)
-    own(1)
-    finish(0)
-
-    def build_g(i):
-        s, half = i % GROUP, i // GROUP
-        t0 = pl.multiple_of(half * 128, 128)
-        v = pltpu.roll(rt[pl.ds(t0, 128), :], (128 - s * 16) % 128, 1)
-        want = lax.broadcasted_iota(jnp.int32, (128, SLOTS), 1).astype(F32) + base
-        sel = jnp.zeros((128, SLOTS), F32)
+    def build_g(i, carry):
+        s, b = i % GROUP, i // GROUP
+        t0 = pl.multiple_of(b * GB, GB)
+        v = pltpu.roll(rt[pl.ds(t0, GB), :], (128 - s * 16) % 128, 1)
+        want = lax.broadcasted_iota(jnp.int32, (GB, SLOTS), 1).astype(F32) + base
+        sel = jnp.zeros((GB, SLOTS), F32)
         for j in range(8):
             sel = jnp.where(v[:, j : j + 1] == want, v[:, 8 + j : 9 + j], sel)
         g1 = (sel * (1.0 - 2.0**-8)).astype(BF16)
@@ -203,23 +202,42 @@
         g2 = rest.astype(BF16)
         g3 = (rest - g2.astype(F32)).astype(BF16)
         for p, part in enumerate((g1, g2, g3)):
-            xall[pl.ds(pl.multiple_of(s * 768 + p * 256 + t0, 128), 128), :] = part
+            gmat[s, pl.ds(pl.multiple_of(p * 256 + t0, GB), GB), :] = part
+        return carry
+
+    lax.fori_loop(0, GROUP * SLOTS // PB, build_p, 0)
+    forward(0)
+    own(2)
+    gn = GROUP * ROWS // GB
+    lax.fori_loop(0, gn // 2, build_g, 0)
+    forward(1)
+    own(3)
+    lax.fori_loop(gn // 2, gn, build_g, 0)
+    finish(0)
 
     def gather_rows(k):
         def body(i, carry):
-            s, m = i // 2, i % 2
-            pm = pmat[pl.ds(pl.multiple_of(i * 256, 256), 256), :]
-            xs = xall[pl.ds(pl.multiple_of((k * GROUP + s) * ROWS, ROWS), ROWS), :]
-            got = jnp.dot(pm, xs, preferred_element_type=F32).astype(BF16)
-            gbuf[s, pl.ds(pl.multiple_of(m * 256, 256), 256), :] = got
+            for s in (2 * i, 2 * i + 1):
+                xs = xall[pl.ds(pl.multiple_of((k * GROUP + s) * ROWS, ROWS), ROWS), :]
+                gbuf[s] = jnp.dot(pmat[s], xs, preferred_element_type=F32).astype(BF16)
             return carry
 
-        lax.fori_loop(0, 2 * GROUP, body, 0)
+        lax.fori_loop(0, GROUP // 2, body, 0)
 
     def block(i, n=1):
         return pl.ds(pl.multiple_of(i * 256, 256), n * 256)
 
-    def experts(k, lo, hi):
+    def down(c, e):
+        i = c * LOCAL + e
+        d_load(i).wait()
+        v = jnp.dot(hbuf[e], dbuf[i % NBD], preferred_element_type=F32).astype(BF16)
+        ybuf[:, pl.ds(pl.multiple_of(e * CAP, CAP), CAP), :] = v.reshape(GROUP, CAP, CC)
+
+        @pl.when(i + NBD < NC * LOCAL)
+        def _():
+            d_load(i + NBD).start()
+
+    def experts(k):
         def body(e, carry):
             i = k * LOCAL + e
             slot = i % NB
@@ -240,7 +258,7 @@
                 if k == NK - 1:
                     hbuf[e, :, n * 256 : (n + 1) * 256] = (jax.nn.silu(vals[0]) * vals[1]).astype(BF16)
             if k == NK - 1:
-                build_g(e)
+                down(0, e)
 
             @pl.when(i + NB < NK * LOCAL)
             def _():
@@ -249,21 +267,16 @@
 
             return carry
 
-        lax.fori_loop(lo, hi, body, 0)
+        lax.fori_loop(0, LOCAL, body, 0)
 
     for k in range(NK):
-        if k == NK - 1:
-            for kk in range(NK - 1):
-                for i in range(8):
-                    send(i, kk).wait_send()
         gather_rows(k)
-        experts(k, 0, 8)
-        if k < NK - 1:
-            forward(k + 1)
-        if k < NK - 2:
-            own(k + 2)
-        experts(k, 8, LOCAL)
-        if k < NK - 1:
+        experts(k)
+        if k + 2 < NK:
+            forward(k + 2)
+        if k + 4 < NK:
+            own(k + 4)
+        if k + 1 < NK:
             finish(k + 1)
 
     for dev in (partner, xn, yn):
@@ -273,8 +286,7 @@
         dx, dy = d % 2, d // 2
         s = ((y + dy) % 2) * 4 + ((x + dx) % 2) * 2 + core
         ys = ybuf[s]
-        gs = xall[pl.ds(pl.multiple_of(s * 768, 256), 768), :]
-        v = jnp.dot(gs, ys, preferred_element_type=F32)
+        v = jnp.dot(gmat[s], ys, preferred_element_type=F32)
         v = v[0:256] + (v[256:512] + v[512:768])
         big[block(to + dx * 2 + dy), :] = v[:, :128]
         big[block(to + 4 + dy * 2 + dx), :] = v[:, 128:]
@@ -309,19 +321,13 @@
         ici(3, c).start()
 
     def column_chunk(c, carry):
-        def down(e, inner):
-            i = c * LOCAL + e
-            d_load(i).wait()
-            v = jnp.dot(hbuf[e], dbuf[i % NBD], preferred_element_type=F32).astype(BF16)
-            ybuf[:, pl.ds(pl.multiple_of(e * CAP, CAP), CAP), :] = v.reshape(GROUP, CAP, CC)
-
-            @pl.when(i + NBD < NC * LOCAL)
-            def _():
-                d_load(i + NBD).start()
-
-            return inner
-
-        lax.fori_loop(0, LOCAL, down, 0)
+        @pl.when(c > 0)
+        def _():
+            def one(e, inner):
+                down(c, e)
+                return inner
+
+            lax.fori_loop(0, LOCAL, one, 0)
 
         @pl.when(c >= 2)
         def _():
@@ -383,8 +389,9 @@
 
     for c in (NC - 2, NC - 1):
         d2d(c).wait_send()
-    for i in range(8):
-        send(i, NK - 1).wait_send()
+    for k in range(NK):
+        for i in range(8):
+            send(i, k).wait_send()
     for d in range(1, GROUP):
         r_copy(d, g, (g + d) % GROUP).wait_send()
 
@@ -401,28 +408,25 @@
         local_experts = w_gate.shape[0]
         slot_count = capacity(rows, top_k, local_experts * group_size)
         assert (rows, width, local_experts, slot_count, group_size) == (ROWS, WIDTH, LOCAL, CAP, GROUP)
-        flat_pos = jnp.where(slot_ids >= 0, expert_ids * slot_count + slot_ids, -1)
-        routing = jnp.concatenate([flat_pos.astype(F32), gate_weights], axis=1).T
-
         vmem = pl.BlockSpec(memory_space=pltpu.VMEM)
         hbm = pl.BlockSpec(memory_space=pl.ANY)
         dma = pltpu.SemaphoreType.DMA
         return pl.pallas_call(
             layer_kernel,
             out_shape=jax.ShapeDtypeStruct((rows, width), BF16),
-            in_specs=[vmem, hbm, hbm, hbm, hbm],
+            in_specs=[vmem, vmem, vmem, hbm, hbm, hbm, hbm],
             out_specs=vmem,
             scratch_shapes=[
                 pltpu.VMEM((GROUP * 16, ROWS), F32),
                 pltpu.VMEM((ROWS, GROUP * 16), F32),
                 pltpu.VMEM((NK * GROUP * ROWS, KC), BF16),
-                pltpu.VMEM((GROUP * SLOTS, ROWS), BF16),
+                pltpu.VMEM((GROUP, SLOTS, ROWS), BF16),
+                pltpu.VMEM((GROUP, 3 * ROWS, SLOTS), BF16),
                 pltpu.VMEM((GROUP, SLOTS, KC), BF16),
                 pltpu.VMEM((NBLK * 256, 128), F32),
                 pltpu.VMEM((NB, 2, KC, FF), BF16),
                 pltpu.VMEM((LOCAL, GROUP * CAP, FF), BF16),
                 pltpu.VMEM((NBD, FF, CC), BF16),
-                pltpu.VMEM((GROUP, SLOTS, CC), BF16),
                 dma((NK,)),
                 dma((GROUP - 1,)),
                 dma((GROUP - 1,)),
@@ -445,6 +449,6 @@
                 transcendentals=LOCAL * GROUP * CAP * FF,
             ),
             name="moe_layer",
-        )(routing, tokens, w_gate, w_up, w_down)
+        )(expert_ids.T, slot_ids.T, gate_weights.T, tokens, w_gate, w_up, w_down)
 
     return jax.shard_map(local_layer, mesh=mesh, in_specs=(tok_spec, tok_spec, tok_spec, tok_spec, weight_spec, weight_spec, weight_spec), out_specs=tok_spec, check_vma=False)

time: 168 us -> 184 us (1.095)
  Pallas kernels: 164 us -> 182 us
  other arithmetic: 2.02 us -> 0 us
    pallas_call x1, Pallas kernels: 164 us -> 182 us  [local_layer(): pl.pallas_call(layer_kernel, out_shape=jax.ShapeDtypeStruct((rows, width)...]
where the time goes in v2:
time: 184 us
  Pallas kernels  182 us (99%)
  local copies, waits for them, and re-layouts  2.3 us (1%)
    pallas_call x1, Pallas kernels, local_layer(): pl.pallas_call(layer_kernel, out_shape=jax.ShapeDtypeStruct((rows, width)...  182 us

profile of v2, /device:TPU:0, one launch (start us, length us, event | category | flops | bytes accessed | tf_op | source)
XLA Modules:
  0.0 184.0 jit_solution(16589949334828620850)
XLA Ops:
  0.0 181.7 %moe_layer.1 = bf16[256,2048]{1,0:T(8,128)(2,1)} custom-call(s32[8,256]{1,0:T(8,128)} %bitcast.3, s32[8,256]{1,0:T(8,128)} %bitcast.4, f32[8,256]{1,0:T(8,128)} %bitcast.5, bf16[256,2048]{1,0:T(8,128)(2,1)} %tok_ref.1, bf16[16,2048,768]{2,1,0:T(8,128)(2,1)} %wg_ref.1, bf16[16,2048,768]{2,1,0:T(8,128)(2,1)} %wu_ref.1, bf16[16,768,2048]{2,1,0:T(8,128)(2,1)} %wd_ref.1), custom_call_target="tpu_custom_call" | custom-call | flops 38654705664 | bytes 150994944 | tf_op jit(solution)/shard_map/moe_layer/pallas_call | solution.py:414
  181.7 2.3 %copy.9 = bf16[256,2048]{1,0:T(8,128)(2,1)} copy(bf16[256,2048]{1,0:T(8,128)(2,1)} %moe_layer.1) | data formatting | bytes 2097152

commit v3 on v2

--- a/solution.py
+++ b/solution.py
@@ -19,10 +19,11 @@
 SLOTS = LOCAL * CAP
 KC = 256
 NK = WIDTH // KC
-NB = 10
+U = 4
+NB = 3
 CC = 256
 NC = WIDTH // CC
-NBD = 8
+NBD = 2
 LAG = 2
 
 OWN = 0
@@ -67,7 +68,7 @@
 
     def own_load(k):
         return pltpu.make_async_copy(
-            tok_ref.at[:, pl.ds(k * KC, KC)],
+            tok_ref.at[:, pl.ds(pl.multiple_of(k * KC, KC), KC)],
             xall.at[pl.ds(pl.multiple_of((k * GROUP + g) * ROWS, ROWS), ROWS), :],
             lsem.at[k],
         )
@@ -75,18 +76,20 @@
     for k in range(NK):
         own_load(k).start()
 
+    steps = LOCAL // U
+
     def w_load(i):
-        k, e, slot = i // LOCAL, i % LOCAL, i % NB
+        k, e, slot = i // steps, (i % steps) * U, i % NB
         rows = pl.ds(pl.multiple_of(k * KC, KC), KC)
         return [
-            pltpu.make_async_copy(ref.at[e, rows, :], wbuf.at[slot, j], w_sem.at[slot, j])
+            pltpu.make_async_copy(ref.at[pl.ds(e, U), rows, :], wbuf.at[slot, j], w_sem.at[slot, j])
             for j, ref in enumerate((wg_ref, wu_ref))
         ]
 
     def d_load(i):
-        c, e, slot = i // LOCAL, i % LOCAL, i % NBD
+        c, e, slot = i // steps, (i % steps) * U, i % NBD
         cols = pl.ds(pl.multiple_of(c * CC, CC), CC)
-        return pltpu.make_async_copy(wd_ref.at[e, :, cols], dbuf.at[slot], d_sem.at[slot])
+        return pltpu.make_async_copy(wd_ref.at[pl.ds(e, U), :, cols], dbuf.at[slot], d_sem.at[slot])
 
     for i in range(NB):
         for cp in w_load(i):
@@ -209,75 +212,98 @@
     forward(0)
     own(2)
     gn = GROUP * ROWS // GB
-    lax.fori_loop(0, gn // 2, build_g, 0)
+    lax.fori_loop(0, gn // 4, build_g, 0)
     forward(1)
     own(3)
-    lax.fori_loop(gn // 2, gn, build_g, 0)
     finish(0)
 
     def gather_rows(k):
         def body(i, carry):
-            for s in (2 * i, 2 * i + 1):
+            for u in range(4):
+                s = 4 * i + u
                 xs = xall[pl.ds(pl.multiple_of((k * GROUP + s) * ROWS, ROWS), ROWS), :]
                 gbuf[s] = jnp.dot(pmat[s], xs, preferred_element_type=F32).astype(BF16)
             return carry
 
-        lax.fori_loop(0, GROUP // 2, body, 0)
+        lax.fori_loop(0, GROUP // 4, body, 0)
 
     def block(i, n=1):
         return pl.ds(pl.multiple_of(i * 256, 256), n * 256)
 
-    def down(c, e):
-        i = c * LOCAL + e
+    def down(c, t):
+        i = c * steps + t
+        slot = i % NBD
         d_load(i).wait()
-        v = jnp.dot(hbuf[e], dbuf[i % NBD], preferred_element_type=F32).astype(BF16)
-        ybuf[:, pl.ds(pl.multiple_of(e * CAP, CAP), CAP), :] = v.reshape(GROUP, CAP, CC)
-
-        @pl.when(i + NBD < NC * LOCAL)
+        rows = pl.ds(pl.multiple_of(t * U * CAP, U * CAP), U * CAP)
+        for u in range(U):
+            v = jnp.dot(hbuf[t * U + u], dbuf[slot, u], preferred_element_type=F32).astype(BF16)
+            ybuf.at[:, rows, :][:, u * CAP : (u + 1) * CAP, :] = v.reshape(GROUP, CAP, CC)
+
+        @pl.when(i + NBD < NC * steps)
         def _():
             d_load(i + NBD).start()
 
-    def experts(k):
-        def body(e, carry):
-            i = k * LOCAL + e
+    def experts(k, first=False, last=False):
+        def body(t, carry):
+            i = k * steps + t
             slot = i % NB
             for cp in w_load(i):
                 cp.wait()
-            lhs = gbuf[:, pl.ds(pl.multiple_of(e * CAP, CAP), CAP), :].reshape(GROUP * CAP, KC)
-            for n in range(FF // 256):
-                vals = []
-                for j in range(2):
-                    v = jnp.dot(lhs, wbuf[slot, j, :, n * 256 : (n + 1) * 256], preferred_element_type=F32)
-                    at = e * 12 + j * 6 + n * 2
-                    if k > 0:
-                        v = v + jnp.concatenate([big[block(at), :], big[block(at + 1), :]], axis=1)
-                    if k < NK - 1:
-                        big[block(at), :] = v[:, :128]
-                        big[block(at + 1), :] = v[:, 128:]
-                    vals.append(v)
-                if k == NK - 1:
-                    hbuf[e, :, n * 256 : (n + 1) * 256] = (jax.nn.silu(vals[0]) * vals[1]).astype(BF16)
-            if k == NK - 1:
-                down(0, e)
-
-            @pl.when(i + NB < NK * LOCAL)
+            lhs4 = gbuf.at[:, pl.ds(pl.multiple_of(t * U * CAP, U * CAP), U * CAP), :]
+            big4 = big.at[block(t * U * 12, U * 12), :]
+            for u in range(U):
+                lhs = lhs4[:, u * CAP : (u + 1) * CAP, :].reshape(GROUP * CAP, KC)
+                for n in range(FF // 256):
+                    vals = []
+                    for j in range(2):
+                        v = jnp.dot(lhs, wbuf[slot, j, u, :, n * 256 : (n + 1) * 256], preferred_element_type=F32)
+                        at = (u * 12 + j * 6 + n * 2) * 256
+                        if not first:
+                            v = v + jnp.concatenate([big4[at : at + 256, :], big4[at + 256 : at + 512, :]], axis=1)
+                        if not last:
+                            big4[at : at + 256, :] = v[:, :128]
+                            big4[at + 256 : at + 512, :] = v[:, 128:]
+                        vals.append(v)
+                    if last:
+                        hbuf[t * U + u, :, n * 256 : (n + 1) * 256] = (jax.nn.silu(vals[0]) * vals[1]).astype(BF16)
+
+            @pl.when(i + NB < NK * steps)
             def _():
                 for cp in w_load(i + NB):
                     cp.start()
 
+            if last:
+                down(0, t)
+
             return carry
 
-        lax.fori_loop(0, LOCAL, body, 0)
-
-    for k in range(NK):
+        lax.fori_loop(0, steps, body, 0)
+
+    gather_rows(0)
+    experts(0, first=True)
+    forward(2)
+    own(4)
+    finish(1)
+
+    def middle(k, carry):
         gather_rows(k)
         experts(k)
-        if k + 2 < NK:
+
+        @pl.when(k + 2 < NK)
+        def _():
             forward(k + 2)
-        if k + 4 < NK:
+
+        @pl.when(k + 4 < NK)
+        def _():
             own(k + 4)
-        if k + 1 < NK:
-            finish(k + 1)
+
+        lax.fori_loop(4 + k * 4, 8 + k * 4, build_g, 0)
+        finish(k + 1)
+        return carry
+
+    lax.fori_loop(1, NK - 1, middle, 0)
+    gather_rows(NK - 1)
+    experts(NK - 1, last=True)
 
     for dev in (partner, xn, yn):
         pl.semaphore_signal(ready, inc=1, device_id=dev, device_id_type=MESH)
@@ -288,8 +314,10 @@
         ys = ybuf[s]
         v = jnp.dot(gmat[s], ys, preferred_element_type=F32)
         v = v[0:256] + (v[256:512] + v[512:768])
-        big[block(to + dx * 2 + dy), :] = v[:, :128]
-        big[block(to + 4 + dy * 2 + dx), :] = v[:, 128:]
+        into = big.at[block(to, 8), :]
+        a, b = (dx * 2 + dy) * 256, (4 + dy * 2 + dx) * 256
+        into[a : a + 256, :] = v[:, :128]
+        into[b : b + 256, :] = v[:, 128:]
 
     def d2d(c):
         return pltpu.make_async_remote_copy(
@@ -323,21 +351,18 @@
     def column_chunk(c, carry):
         @pl.when(c > 0)
         def _():
-            def one(e, inner):
-                down(c, e)
+            def one(t, inner):
+                down(c, t)
                 return inner
 
-            lax.fori_loop(0, LOCAL, one, 0)
+            lax.fori_loop(0, steps, one, 0)
 
         @pl.when(c >= 2)
         def _():
             d2d(c - 2).wait_send()
 
-        def theirs(d, inner):
+        for d in range(4):
             part(1 - q, d, PBUF + (c % 2) * 8)
-            return inner
-
-        lax.fori_loop(0, 4, theirs, 0)
 
         @pl.when(c == 0)
         def _():
@@ -345,11 +370,8 @@
 
         d2d(c).start()
 
-        def ours(d, inner):
+        for d in range(4):
             part(q, d, OWN + c * 8)
-            return inner
-
-        lax.fori_loop(0, 4, ours, 0)
 
         @pl.when(c >= LAG)
         def _():
@@ -424,9 +446,9 @@
                 pltpu.VMEM((GROUP, 3 * ROWS, SLOTS), BF16),
                 pltpu.VMEM((GROUP, SLOTS, KC), BF16),
                 pltpu.VMEM((NBLK * 256, 128), F32),
-                pltpu.VMEM((NB, 2, KC, FF), BF16),
+                pltpu.VMEM((NB, 2, U, KC, FF), BF16),
                 pltpu.VMEM((LOCAL, GROUP * CAP, FF), BF16),
-                pltpu.VMEM((NBD, FF, CC), BF16),
+                pltpu.VMEM((NBD, U, FF, CC), BF16),
                 dma((NK,)),
                 dma((GROUP - 1,)),
                 dma((GROUP - 1,)),

time: 184 us -> 154 us (0.84)
  Pallas kernels: 182 us -> 151 us
    pallas_call x1, Pallas kernels: 182 us -> 151 us  [local_layer(): pl.pallas_call(layer_kernel, out_shape=jax.ShapeDtypeStruct((rows, width)...]
where the time goes in v3:
time: 154 us
  Pallas kernels  151 us (98%)
  local copies, waits for them, and re-layouts  2.3 us (1%)
    pallas_call x1, Pallas kernels, local_layer(): pl.pallas_call(layer_kernel, out_shape=jax.ShapeDtypeStruct((rows, width)...  151 us

profile of v3, /device:TPU:0, one launch (start us, length us, event | category | flops | bytes accessed | tf_op | source)
XLA Modules:
  0.0 153.8 jit_solution(2150016596191555677)
XLA Ops:
  0.0 151.4 %moe_layer.1 = bf16[256,2048]{1,0:T(8,128)(2,1)} custom-call(s32[8,256]{1,0:T(8,128)} %bitcast.3, s32[8,256]{1,0:T(8,128)} %bitcast.4, f32[8,256]{1,0:T(8,128)} %bitcast.5, bf16[256,2048]{1,0:T(8,128)(2,1)} %tok_ref.1, bf16[16,2048,768]{2,1,0:T(8,128)(2,1)} %wg_ref.1, bf16[16,2048,768]{2,1,0:T(8,128)(2,1)} %wu_ref.1, bf16[16,768,2048]{2,1,0:T(8,128)(2,1)} %wd_ref.1), custom_call_target="tpu_custom_call" | custom-call | flops 38654705664 | bytes 150994944 | tf_op jit(solution)/shard_map/moe_layer/pallas_call | solution.py:436
  151.5 2.3 %copy.9 = bf16[256,2048]{1,0:T(8,128)(2,1)} copy(bf16[256,2048]{1,0:T(8,128)(2,1)} %moe_layer.1) | data formatting | bytes 2097152

commit v4 on v3

--- a/solution.py
+++ b/solution.py
@@ -218,14 +218,9 @@
     finish(0)
 
     def gather_rows(k):
-        def body(i, carry):
-            for u in range(4):
-                s = 4 * i + u
-                xs = xall[pl.ds(pl.multiple_of((k * GROUP + s) * ROWS, ROWS), ROWS), :]
-                gbuf[s] = jnp.dot(pmat[s], xs, preferred_element_type=F32).astype(BF16)
-            return carry
-
-        lax.fori_loop(0, GROUP // 4, body, 0)
+        for s in range(GROUP):
+            xs = xall[pl.ds(pl.multiple_of((k * GROUP + s) * ROWS, ROWS), ROWS), :]
+            gbuf[s] = jnp.dot(pmat[s], xs, preferred_element_type=F32).astype(BF16)
 
     def block(i, n=1):
         return pl.ds(pl.multiple_of(i * 256, 256), n * 256)
@@ -274,6 +269,8 @@
 
             if last:
                 down(0, t)
+            elif not first:
+                build_g(4 + k * 4 + t, 0)
 
             return carry
 
@@ -297,7 +294,6 @@
         def _():
             own(k + 4)
 
-        lax.fori_loop(4 + k * 4, 8 + k * 4, build_g, 0)
         finish(k + 1)
         return carry
 

time: 154 us -> 148 us (0.961)
  Pallas kernels: 151 us -> 145 us
    pallas_call x1, Pallas kernels: 151 us -> 145 us  [local_layer(): pl.pallas_call(layer_kernel, out_shape=jax.ShapeDtypeStruct((rows, width)...]
where the time goes in v4:
time: 148 us; the launch traced here: 147 us
  Pallas kernels  145 us (98%)
  local copies, waits for them, and re-layouts  2.3 us (2%)
    pallas_call x1, Pallas kernels, local_layer(): pl.pallas_call(layer_kernel, out_shape=jax.ShapeDtypeStruct((rows, width)...  145 us

profile of v4, /device:TPU:0, one launch (start us, length us, event | category | flops | bytes accessed | tf_op | source)
XLA Modules:
  0.0 147.4 jit_solution(11518671100039756781)
XLA Ops:
  0.0 145.1 %moe_layer.1 = bf16[256,2048]{1,0:T(8,128)(2,1)} custom-call(s32[8,256]{1,0:T(8,128)} %bitcast.3, s32[8,256]{1,0:T(8,128)} %bitcast.4, f32[8,256]{1,0:T(8,128)} %bitcast.5, bf16[256,2048]{1,0:T(8,128)(2,1)} %tok_ref.1, bf16[16,2048,768]{2,1,0:T(8,128)(2,1)} %wg_ref.1, bf16[16,2048,768]{2,1,0:T(8,128)(2,1)} %wu_ref.1, bf16[16,768,2048]{2,1,0:T(8,128)(2,1)} %wd_ref.1), custom_call_target="tpu_custom_call" | custom-call | flops 38654705664 | bytes 150994944 | tf_op jit(solution)/shard_map/moe_layer/pallas_call | solution.py:432
  145.1 2.3 %copy.9 = bf16[256,2048]{1,0:T(8,128)(2,1)} copy(bf16[256,2048]{1,0:T(8,128)(2,1)} %moe_layer.1) | data formatting | bytes 2097152

commit v5 on v4

--- a/solution.py
+++ b/solution.py
@@ -82,20 +82,25 @@
         k, e, slot = i // steps, (i % steps) * U, i % NB
         rows = pl.ds(pl.multiple_of(k * KC, KC), KC)
         return [
-            pltpu.make_async_copy(ref.at[pl.ds(e, U), rows, :], wbuf.at[slot, j], w_sem.at[slot, j])
+            pltpu.make_async_copy(ref.at[e + u, rows, :], wbuf.at[slot, j, u], w_sem.at[slot, j, u])
+            for u in range(U)
             for j, ref in enumerate((wg_ref, wu_ref))
         ]
 
     def d_load(i):
         c, e, slot = i // steps, (i % steps) * U, i % NBD
         cols = pl.ds(pl.multiple_of(c * CC, CC), CC)
-        return pltpu.make_async_copy(wd_ref.at[pl.ds(e, U), :, cols], dbuf.at[slot], d_sem.at[slot])
+        return [
+            pltpu.make_async_copy(wd_ref.at[e + u, :, cols], dbuf.at[slot, u], d_sem.at[slot, u])
+            for u in range(U)
+        ]
 
     for i in range(NB):
         for cp in w_load(i):
             cp.start()
     for i in range(NBD):
-        d_load(i).start()
+        for cp in d_load(i):
+            cp.start()
 
     mine = pl.multiple_of(g * 16, 16)
     flat_pos = jnp.where(slot_ref[...] >= 0, id_ref[...] * CAP + slot_ref[...], -1)
@@ -228,7 +233,8 @@
     def down(c, t):
         i = c * steps + t
         slot = i % NBD
-        d_load(i).wait()
+        for cp in d_load(i):
+            cp.wait()
         rows = pl.ds(pl.multiple_of(t * U * CAP, U * CAP), U * CAP)
         for u in range(U):
             v = jnp.dot(hbuf[t * U + u], dbuf[slot, u], preferred_element_type=F32).astype(BF16)
@@ -236,7 +242,8 @@
 
         @pl.when(i + NBD < NC * steps)
         def _():
-            d_load(i + NBD).start()
+            for cp in d_load(i + NBD):
+                cp.start()
 
     def experts(k, first=False, last=False):
         def body(t, carry):
@@ -450,8 +457,8 @@
                 dma((GROUP - 1,)),
                 dma((8, NK)),
                 dma((8, NK)),
-                dma((NB, 2)),
-                dma((NBD,)),
+                dma((NB, 2, U)),
+                dma((NBD, U)),
                 dma((NC,)),
                 dma((NC,)),
                 dma((4, NC)),

time: 148 us -> 148 us (level)
  no operation moved by 1% of the time
where the time goes in v5:
time: 148 us
  Pallas kernels  146 us (99%)
  local copies, waits for them, and re-layouts  2.3 us (2%)
    pallas_call x1, Pallas kernels, local_layer(): pl.pallas_call(layer_kernel, out_shape=jax.ShapeDtypeStruct((rows, width)...  146 us

profile of v5, /device:TPU:0, one launch (start us, length us, event | category | flops | bytes accessed | tf_op | source)
XLA Modules:
  0.0 147.9 jit_solution(9846287657543587999)
XLA Ops:
  0.0 145.6 %moe_layer.1 = bf16[256,2048]{1,0:T(8,128)(2,1)} custom-call(s32[8,256]{1,0:T(8,128)} %bitcast.3, s32[8,256]{1,0:T(8,128)} %bitcast.4, f32[8,256]{1,0:T(8,128)} %bitcast.5, bf16[256,2048]{1,0:T(8,128)(2,1)} %tok_ref.1, bf16[16,2048,768]{2,1,0:T(8,128)(2,1)} %wg_ref.1, bf16[16,2048,768]{2,1,0:T(8,128)(2,1)} %wu_ref.1, bf16[16,768,2048]{2,1,0:T(8,128)(2,1)} %wd_ref.1), custom_call_target="tpu_custom_call" | custom-call | flops 38654705664 | bytes 150994944 | tf_op jit(solution)/shard_map/moe_layer/pallas_call | solution.py:439
  145.6 2.3 %copy.9 = bf16[256,2048]{1,0:T(8,128)(2,1)} copy(bf16[256,2048]{1,0:T(8,128)(2,1)} %moe_layer.1) | data formatting | bytes 2097152

commit v6 on v4

--- a/solution.py
+++ b/solution.py
@@ -163,10 +163,12 @@
         send(5, k).start()
         send(6, k).start()
 
-    def finish(k):
+    def diagonal(k):
         arrival(3, k).wait_recv()
         arrival(5, k).wait_recv()
         send(7, k).start()
+
+    def finish(k):
         for i in (0, 4, 6, 7):
             arrival(i, k).wait_recv()
 
@@ -215,6 +217,7 @@
     lax.fori_loop(0, gn // 4, build_g, 0)
     forward(1)
     own(3)
+    diagonal(0)
     finish(0)
 
     def gather_rows(k):
@@ -269,8 +272,21 @@
 
             if last:
                 down(0, t)
-            elif not first:
-                build_g(4 + k * 4 + t, 0)
+            else:
+                if not first:
+                    build_g(4 + k * 4 + t, 0)
+
+                @pl.when(jnp.logical_and(t == 0, k + 2 < NK))
+                def _():
+                    forward(k + 2)
+
+                @pl.when(jnp.logical_and(t == 0, k + 4 < NK))
+                def _():
+                    own(k + 4)
+
+                @pl.when(t == 2)
+                def _():
+                    diagonal(k + 1)
 
             return carry
 
@@ -278,21 +294,11 @@
 
     gather_rows(0)
     experts(0, first=True)
-    forward(2)
-    own(4)
     finish(1)
 
     def middle(k, carry):
         gather_rows(k)
         experts(k)
-
-        @pl.when(k + 2 < NK)
-        def _():
-            forward(k + 2)
-
-        @pl.when(k + 4 < NK)
-        def _():
-            own(k + 4)
 
         finish(k + 1)
         return carry

time: 148 us -> 139 us (0.939)
  Pallas kernels: 145 us -> 136 us
    pallas_call x1, Pallas kernels: 145 us -> 136 us  [local_layer(): pl.pallas_call(layer_kernel, out_shape=jax.ShapeDtypeStruct((rows, width)...]
where the time goes in v6:
time: 139 us; the launch traced here: 138 us
  Pallas kernels  136 us (98%)
  local copies, waits for them, and re-layouts  2.3 us (2%)
    pallas_call x1, Pallas kernels, local_layer(): pl.pallas_call(layer_kernel, out_shape=jax.ShapeDtypeStruct((rows, width)...  136 us

profile of v6, /device:TPU:0, one launch (start us, length us, event | category | flops | bytes accessed | tf_op | source)
XLA Modules:
  0.0 138.4 jit_solution(9704436509949784462)
XLA Ops:
  0.0 136.1 %moe_layer.1 = bf16[256,2048]{1,0:T(8,128)(2,1)} custom-call(s32[8,256]{1,0:T(8,128)} %bitcast.3, s32[8,256]{1,0:T(8,128)} %bitcast.4, f32[8,256]{1,0:T(8,128)} %bitcast.5, bf16[256,2048]{1,0:T(8,128)(2,1)} %tok_ref.1, bf16[16,2048,768]{2,1,0:T(8,128)(2,1)} %wg_ref.1, bf16[16,2048,768]{2,1,0:T(8,128)(2,1)} %wu_ref.1, bf16[16,768,2048]{2,1,0:T(8,128)(2,1)} %wd_ref.1), custom_call_target="tpu_custom_call" | custom-call | flops 38654705664 | bytes 150994944 | tf_op jit(solution)/shard_map/moe_layer/pallas_call | solution.py:438
  136.1 2.3 %copy.9 = bf16[256,2048]{1,0:T(8,128)(2,1)} copy(bf16[256,2048]{1,0:T(8,128)(2,1)} %moe_layer.1) | data formatting | bytes 2097152

commit v7 on v6

--- a/solution.py
+++ b/solution.py
@@ -21,6 +21,7 @@
 NK = WIDTH // KC
 U = 4
 NB = 3
+NX = 2
 CC = 256
 NC = WIDTH // CC
 NBD = 2
@@ -42,9 +43,9 @@
 
 def layer_kernel(
     id_ref, slot_ref, gate_ref, tok_ref, wg_ref, wu_ref, wd_ref, out_ref,
-    rall, rt, xall, pmat, gmat, gbuf, big, wbuf, hbuf, dbuf,
+    rall, rt, xall, pmat, gmat, gbuf, big, wbuf, dbuf, obuf,
     lsem, rs_sem, rr_sem, xs_sem, xr_sem, w_sem, d_sem,
-    ds_sem, dr_sem, is_sem, ir_sem, ready,
+    ds_sem, dr_sem, is_sem, ir_sem, o_sem, ready,
 ):
     data = lax.axis_index("data")
     y = lax.axis_index("node")
@@ -78,11 +79,17 @@
 
     steps = LOCAL // U
 
+    tail_step = (NK - 1) * steps
+    hidden = 2 * U * NB
+
+    def w_slot(i):
+        return jnp.where(i < tail_step, i % (NB + NX), (i - tail_step) % NB) * (2 * U)
+
     def w_load(i):
-        k, e, slot = i // steps, (i % steps) * U, i % NB
+        k, e, at = i // steps, (i % steps) * U, w_slot(i)
         rows = pl.ds(pl.multiple_of(k * KC, KC), KC)
         return [
-            pltpu.make_async_copy(ref.at[pl.ds(e, U), rows, :], wbuf.at[slot, j], w_sem.at[slot, j])
+            pltpu.make_async_copy(ref.at[pl.ds(e, U), rows, :], wbuf.at[pl.ds(at + j * U, U)], w_sem.at[at // (2 * U), j])
             for j, ref in enumerate((wg_ref, wu_ref))
         ]
 
@@ -91,7 +98,7 @@
         cols = pl.ds(pl.multiple_of(c * CC, CC), CC)
         return pltpu.make_async_copy(wd_ref.at[pl.ds(e, U), :, cols], dbuf.at[slot], d_sem.at[slot])
 
-    for i in range(NB):
+    for i in range(NB + NX):
         for cp in w_load(i):
             cp.start()
     for i in range(NBD):
@@ -234,7 +241,7 @@
         d_load(i).wait()
         rows = pl.ds(pl.multiple_of(t * U * CAP, U * CAP), U * CAP)
         for u in range(U):
-            v = jnp.dot(hbuf[t * U + u], dbuf[slot, u], preferred_element_type=F32).astype(BF16)
+            v = jnp.dot(wbuf[hidden + t * U + u], dbuf[slot, u], preferred_element_type=F32).astype(BF16)
             ybuf.at[:, rows, :][:, u * CAP : (u + 1) * CAP, :] = v.reshape(GROUP, CAP, CC)
 
         @pl.when(i + NBD < NC * steps)
@@ -244,9 +251,9 @@
     def experts(k, first=False, last=False):
         def body(t, carry):
             i = k * steps + t
-            slot = i % NB
             for cp in w_load(i):
                 cp.wait()
+            w4 = wbuf.at[pl.ds(w_slot(i), 2 * U)]
             lhs4 = gbuf.at[:, pl.ds(pl.multiple_of(t * U * CAP, U * CAP), U * CAP), :]
             big4 = big.at[block(t * U * 12, U * 12), :]
             for u in range(U):
@@ -254,7 +261,7 @@
                 for n in range(FF // 256):
                     vals = []
                     for j in range(2):
-                        v = jnp.dot(lhs, wbuf[slot, j, u, :, n * 256 : (n + 1) * 256], preferred_element_type=F32)
+                        v = jnp.dot(lhs, w4[j * U + u, :, n * 256 : (n + 1) * 256], preferred_element_type=F32)
                         at = (u * 12 + j * 6 + n * 2) * 256
                         if not first:
                             v = v + jnp.concatenate([big4[at : at + 256, :], big4[at + 256 : at + 512, :]], axis=1)
@@ -263,9 +270,14 @@
                             big4[at + 256 : at + 512, :] = v[:, 128:]
                         vals.append(v)
                     if last:
-                        hbuf[t * U + u, :, n * 256 : (n + 1) * 256] = (jax.nn.silu(vals[0]) * vals[1]).astype(BF16)
-
-            @pl.when(i + NB < NK * steps)
+                        wbuf[hidden + t * U + u, :, n * 256 : (n + 1) * 256] = (jax.nn.silu(vals[0]) * vals[1]).astype(BF16)
+
+            @pl.when(i + NB + NX < tail_step)
+            def _():
+                for cp in w_load(i + NB + NX):
+                    cp.start()
+
+            @pl.when(jnp.logical_and(i + NB >= tail_step, i + NB < NK * steps))
             def _():
                 for cp in w_load(i + NB):
                     cp.start()
@@ -321,13 +333,20 @@
         into[a : a + 256, :] = v[:, :128]
         into[b : b + 256, :] = v[:, 128:]
 
-    def d2d(c):
+    def d2d(i, c):
+        at = (2, 6, 0, 4)[i]
         return pltpu.make_async_remote_copy(
-            src_ref=big.at[block(PBUF + (c % 2) * 8, 8), :],
-            dst_ref=big.at[block(DRECV + c * 8, 8), :],
-            send_sem=ds_sem.at[c], recv_sem=dr_sem.at[c],
+            src_ref=big.at[block(PBUF + (c % 2) * 8 + at, 2), :],
+            dst_ref=big.at[block(DRECV + c * 8 + at, 2), :],
+            send_sem=ds_sem.at[i, c], recv_sem=dr_sem.at[i, c],
             device_id=partner, device_id_type=MESH,
         )
+
+    def pair_sum(i, c):
+        at = (2, 6, 0, 4)[i]
+        d2d(i, c).wait_recv()
+        rows = block(OWN + c * 8 + at, 2)
+        big[rows, :] = big[rows, :] + big[block(DRECV + c * 8 + at, 2), :]
 
     def ici(i, c):
         src, dst, n, dev = (
@@ -361,33 +380,31 @@
 
         @pl.when(c >= 2)
         def _():
-            d2d(c - 2).wait_send()
-
-        for d in range(4):
+            for i in range(4):
+                d2d(i, c - 2).wait_send()
+
+        for d in (3, 1, 2, 0):
             part(1 - q, d, PBUF + (c % 2) * 8)
 
         @pl.when(c == 0)
         def _():
             pl.semaphore_wait(ready, 3)
 
-        d2d(c).start()
-
-        for d in range(4):
+        for i in range(4):
+            d2d(i, c).start()
+        for d in (3, 1, 2, 0):
             part(q, d, OWN + c * 8)
 
         @pl.when(c >= LAG)
         def _():
             second_hop(c - LAG)
 
-        d2d(c).wait_recv()
-
-        def add(b, inner):
-            big[block(OWN + c * 8 + b), :] = big[block(OWN + c * 8 + b), :] + big[block(DRECV + c * 8 + b), :]
-            return inner
-
-        lax.fori_loop(0, 8, add, 0)
+        pair_sum(0, c)
         ici(0, c).start()
+        pair_sum(1, c)
         ici(1, c).start()
+        pair_sum(2, c)
+        pair_sum(3, c)
         return carry
 
     lax.fori_loop(0, NC, column_chunk, 0)
@@ -397,22 +414,30 @@
         return carry
 
     lax.fori_loop(NC - LAG, NC, tail, 0)
+
+    def out_copy(c):
+        cols = pl.ds(pl.multiple_of(c * CC, CC), CC)
+        return pltpu.make_async_copy(obuf.at[c], out_ref.at[:, cols], o_sem.at[c])
 
     def final(c, carry):
         ici(2, c).wait_recv()
         a = big[block(OWN + c * 8), :] + big[block(RA1 + c * 2), :] + big[block(RA2 + c), :]
         ici(3, c).wait_recv()
         b = big[block(OWN + c * 8 + 4), :] + big[block(RB1 + c * 2), :] + big[block(RB2 + c), :]
-        out_ref[:, pl.ds(pl.multiple_of(c * CC, CC), 128)] = a.astype(BF16)
-        out_ref[:, pl.ds(pl.multiple_of(c * CC + 128, 128), 128)] = b.astype(BF16)
+        obuf[c, :, 0:128] = a.astype(BF16)
+        obuf[c, :, 128:256] = b.astype(BF16)
+        out_copy(c).start()
         for i in range(4):
             ici(i, c).wait_send()
         return carry
 
     lax.fori_loop(0, NC, final, 0)
 
+    for c in range(NC):
+        out_copy(c).wait()
     for c in (NC - 2, NC - 1):
-        d2d(c).wait_send()
+        for i in range(4):
+            d2d(i, c).wait_send()
     for k in range(NK):
         for i in range(8):
             send(i, k).wait_send()
@@ -439,7 +464,7 @@
             layer_kernel,
             out_shape=jax.ShapeDtypeStruct((rows, width), BF16),
             in_specs=[vmem, vmem, vmem, hbm, hbm, hbm, hbm],
-            out_specs=vmem,
+            out_specs=hbm,
             scratch_shapes=[
                 pltpu.VMEM((GROUP * 16, ROWS), F32),
                 pltpu.VMEM((ROWS, GROUP * 16), F32),
@@ -448,20 +473,21 @@
                 pltpu.VMEM((GROUP, 3 * ROWS, SLOTS), BF16),
                 pltpu.VMEM((GROUP, SLOTS, KC), BF16),
                 pltpu.VMEM((NBLK * 256, 128), F32),
-                pltpu.VMEM((NB, 2, U, KC, FF), BF16),
-                pltpu.VMEM((LOCAL, GROUP * CAP, FF), BF16),
+                pltpu.VMEM((2 * U * (NB + NX), KC, FF), BF16),
                 pltpu.VMEM((NBD, U, FF, CC), BF16),
+                pltpu.VMEM((NC, ROWS, CC), BF16),
                 dma((NK,)),
                 dma((GROUP - 1,)),
                 dma((GROUP - 1,)),
                 dma((8, NK)),
                 dma((8, NK)),
-                dma((NB, 2)),
+                dma((NB + NX, 2)),
                 dma((NBD,)),
-                dma((NC,)),
-                dma((NC,)),
                 dma((4, NC)),
                 dma((4, NC)),
+                dma((4, NC)),
+                dma((4, NC)),
+                dma((NC,)),
                 pltpu.SemaphoreType.REGULAR,
             ],
             compiler_params=pltpu.CompilerParams(

time: 139 us -> 146 us (1.050)
  Pallas kernels: 136 us -> 143 us
    pallas_call x1, Pallas kernels: 136 us -> 143 us  [local_layer(): pl.pallas_call(layer_kernel, out_shape=jax.ShapeDtypeStruct((rows, width)...]
where the time goes in v7:
time: 146 us; the launch traced here: 145 us
  Pallas kernels  143 us (98%)
  local copies, waits for them, and re-layouts  2.3 us (2%)
    pallas_call x1, Pallas kernels, local_layer(): pl.pallas_call(layer_kernel, out_shape=jax.ShapeDtypeStruct((rows, width)...  143 us

profile of v7, /device:TPU:0, one launch (start us, length us, event | category | flops | bytes accessed | tf_op | source)
XLA Modules:
  0.0 145.5 jit_solution(4016961457724318036)
XLA Ops:
  0.0 143.1 %moe_layer.1 = bf16[256,2048]{1,0:T(8,128)(2,1)} custom-call(s32[8,256]{1,0:T(8,128)} %bitcast.3, s32[8,256]{1,0:T(8,128)} %bitcast.4, f32[8,256]{1,0:T(8,128)} %bitcast.5, bf16[256,2048]{1,0:T(8,128)(2,1)} %tok_ref.1, bf16[16,2048,768]{2,1,0:T(8,128)(2,1)} %wg_ref.1, bf16[16,2048,768]{2,1,0:T(8,128)(2,1)} %wu_ref.1, bf16[16,768,2048]{2,1,0:T(8,128)(2,1)} %wd_ref.1), custom_call_target="tpu_custom_call" | custom-call | flops 38654705664 | bytes 150994944 | tf_op jit(solution)/shard_map/moe_layer/pallas_call | solution.py:463
  143.2 2.3 %copy.9 = bf16[256,2048]{1,0:T(8,128)(2,1)} copy(bf16[256,2048]{1,0:T(8,128)(2,1)} %moe_layer.1) | data formatting | bytes 2097152

commit v8 on v7

--- a/solution.py
+++ b/solution.py
@@ -20,8 +20,7 @@
 KC = 256
 NK = WIDTH // KC
 U = 4
-NB = 3
-NX = 2
+NB = 5
 CC = 256
 NC = WIDTH // CC
 NBD = 2
@@ -79,17 +78,11 @@
 
     steps = LOCAL // U
 
-    tail_step = (NK - 1) * steps
-    hidden = 2 * U * NB
-
-    def w_slot(i):
-        return jnp.where(i < tail_step, i % (NB + NX), (i - tail_step) % NB) * (2 * U)
-
     def w_load(i):
-        k, e, at = i // steps, (i % steps) * U, w_slot(i)
+        k, e, slot = i // steps, (i % steps) * U, i % NB
         rows = pl.ds(pl.multiple_of(k * KC, KC), KC)
         return [
-            pltpu.make_async_copy(ref.at[pl.ds(e, U), rows, :], wbuf.at[pl.ds(at + j * U, U)], w_sem.at[at // (2 * U), j])
+            pltpu.make_async_copy(ref.at[pl.ds(e, U), rows, :], wbuf.at[slot, j], w_sem.at[slot, j])
             for j, ref in enumerate((wg_ref, wu_ref))
         ]
 
@@ -98,7 +91,7 @@
         cols = pl.ds(pl.multiple_of(c * CC, CC), CC)
         return pltpu.make_async_copy(wd_ref.at[pl.ds(e, U), :, cols], dbuf.at[slot], d_sem.at[slot])
 
-    for i in range(NB + NX):
+    for i in range(NB):
         for cp in w_load(i):
             cp.start()
     for i in range(NBD):
@@ -240,8 +233,10 @@
         slot = i % NBD
         d_load(i).wait()
         rows = pl.ds(pl.multiple_of(t * U * CAP, U * CAP), U * CAP)
+        h4 = xall.at[block(t * U * 3, U * 3), :]
         for u in range(U):
-            v = jnp.dot(wbuf[hidden + t * U + u], dbuf[slot, u], preferred_element_type=F32).astype(BF16)
+            h = jnp.concatenate([h4[(u * 3 + n) * 256 : (u * 3 + n + 1) * 256, :] for n in range(3)], axis=1)
+            v = jnp.dot(h, dbuf[slot, u], preferred_element_type=F32).astype(BF16)
             ybuf.at[:, rows, :][:, u * CAP : (u + 1) * CAP, :] = v.reshape(GROUP, CAP, CC)
 
         @pl.when(i + NBD < NC * steps)
@@ -253,15 +248,16 @@
             i = k * steps + t
             for cp in w_load(i):
                 cp.wait()
-            w4 = wbuf.at[pl.ds(w_slot(i), 2 * U)]
+            w4 = wbuf.at[i % NB]
             lhs4 = gbuf.at[:, pl.ds(pl.multiple_of(t * U * CAP, U * CAP), U * CAP), :]
+            h4 = xall.at[block(t * U * 3, U * 3), :]
             big4 = big.at[block(t * U * 12, U * 12), :]
             for u in range(U):
                 lhs = lhs4[:, u * CAP : (u + 1) * CAP, :].reshape(GROUP * CAP, KC)
                 for n in range(FF // 256):
                     vals = []
                     for j in range(2):
-                        v = jnp.dot(lhs, w4[j * U + u, :, n * 256 : (n + 1) * 256], preferred_element_type=F32)
+                        v = jnp.dot(lhs, w4[j, u, :, n * 256 : (n + 1) * 256], preferred_element_type=F32)
                         at = (u * 12 + j * 6 + n * 2) * 256
                         if not first:
                             v = v + jnp.concatenate([big4[at : at + 256, :], big4[at + 256 : at + 512, :]], axis=1)
@@ -270,14 +266,9 @@
                             big4[at + 256 : at + 512, :] = v[:, 128:]
                         vals.append(v)
                     if last:
-                        wbuf[hidden + t * U + u, :, n * 256 : (n + 1) * 256] = (jax.nn.silu(vals[0]) * vals[1]).astype(BF16)
-
-            @pl.when(i + NB + NX < tail_step)
-            def _():
-                for cp in w_load(i + NB + NX):
-                    cp.start()
-
-            @pl.when(jnp.logical_and(i + NB >= tail_step, i + NB < NK * steps))
+                        h4[(u * 3 + n) * 256 : (u * 3 + n + 1) * 256, :] = (jax.nn.silu(vals[0]) * vals[1]).astype(BF16)
+
+            @pl.when(i + NB < NK * steps)
             def _():
                 for cp in w_load(i + NB):
                     cp.start()
@@ -316,6 +307,9 @@
         return carry
 
     lax.fori_loop(1, NK - 1, middle, 0)
+    for k in range(6):
+        for i in range(8):
+            send(i, k).wait_send()
     gather_rows(NK - 1)
     experts(NK - 1, last=True)
 
@@ -438,7 +432,7 @@
     for c in (NC - 2, NC - 1):
         for i in range(4):
             d2d(i, c).wait_send()
-    for k in range(NK):
+    for k in range(6, NK):
         for i in range(8):
             send(i, k).wait_send()
     for d in range(1, GROUP):
@@ -473,7 +467,7 @@
                 pltpu.VMEM((GROUP, 3 * ROWS, SLOTS), BF16),
                 pltpu.VMEM((GROUP, SLOTS, KC), BF16),
                 pltpu.VMEM((NBLK * 256, 128), F32),
-                pltpu.VMEM((2 * U * (NB + NX), KC, FF), BF16),
+                pltpu.VMEM((NB, 2, U, KC, FF), BF16),
                 pltpu.VMEM((NBD, U, FF, CC), BF16),
                 pltpu.VMEM((NC, ROWS, CC), BF16),
                 dma((NK,)),
@@ -481,7 +475,7 @@
                 dma((GROUP - 1,)),
                 dma((8, NK)),
                 dma((8, NK)),
-                dma((NB + NX, 2)),
+                dma((NB, 2)),
                 dma((NBD,)),
                 dma((4, NC)),
                 dma((4, NC)),

time: 146 us -> 138 us (0.945)
  Pallas kernels: 143 us -> 136 us
    pallas_call x1, Pallas kernels: 143 us -> 136 us  [local_layer(): pl.pallas_call(layer_kernel, out_shape=jax.ShapeDtypeStruct((rows, width)...]
where the time goes in v8:
time: 138 us
  Pallas kernels  136 us (99%)
  local copies, waits for them, and re-layouts  2.3 us (2%)
    pallas_call x1, Pallas kernels, local_layer(): pl.pallas_call(layer_kernel, out_shape=jax.ShapeDtypeStruct((rows, width)...  136 us

profile of v8, /device:TPU:0, one launch (start us, length us, event | category | flops | bytes accessed | tf_op | source)
XLA Modules:
  0.0 137.9 jit_solution(4611569181197673835)
XLA Ops:
  0.0 135.6 %moe_layer.1 = bf16[256,2048]{1,0:T(8,128)(2,1)} custom-call(s32[8,256]{1,0:T(8,128)} %bitcast.3, s32[8,256]{1,0:T(8,128)} %bitcast.4, f32[8,256]{1,0:T(8,128)} %bitcast.5, bf16[256,2048]{1,0:T(8,128)(2,1)} %tok_ref.1, bf16[16,2048,768]{2,1,0:T(8,128)(2,1)} %wg_ref.1, bf16[16,2048,768]{2,1,0:T(8,128)(2,1)} %wu_ref.1, bf16[16,768,2048]{2,1,0:T(8,128)(2,1)} %wd_ref.1), custom_call_target="tpu_custom_call" | custom-call | flops 38654705664 | bytes 150994944 | tf_op jit(solution)/shard_map/moe_layer/pallas_call | solution.py:457
  135.6 2.3 %copy.9 = bf16[256,2048]{1,0:T(8,128)(2,1)} copy(bf16[256,2048]{1,0:T(8,128)(2,1)} %moe_layer.1) | data formatting | bytes 2097152

commit v9 on v8

--- a/solution.py
+++ b/solution.py
@@ -244,11 +244,44 @@
             d_load(i + NBD).start()
 
     def experts(k, first=False, last=False):
-        def body(t, carry):
-            i = k * steps + t
-            for cp in w_load(i):
-                cp.wait()
-            w4 = wbuf.at[i % NB]
+        wide = 1 if last else 2
+
+        def body(tt, carry):
+            i = k * steps + tt * wide
+            for w in range(wide):
+                for cp in w_load(i + w):
+                    cp.wait()
+            for w in range(wide):
+                one_step(tt * wide + w, wbuf.at[(i + w) % NB])
+            for w in range(wide):
+
+                @pl.when(i + w + NB < NK * steps)
+                def _():
+                    for cp in w_load(i + w + NB):
+                        cp.start()
+
+            if last:
+                down(0, tt)
+            else:
+                if not first:
+                    for w in range(wide):
+                        build_g(4 + k * 4 + tt * wide + w, 0)
+
+                @pl.when(jnp.logical_and(tt == 0, k + 2 < NK))
+                def _():
+                    forward(k + 2)
+
+                @pl.when(jnp.logical_and(tt == 0, k + 4 < NK))
+                def _():
+                    own(k + 4)
+
+                @pl.when(tt == 0)
+                def _():
+                    diagonal(k + 1)
+
+            return carry
+
+        def one_step(t, w4):
             lhs4 = gbuf.at[:, pl.ds(pl.multiple_of(t * U * CAP, U * CAP), U * CAP), :]
             h4 = xall.at[block(t * U * 3, U * 3), :]
             big4 = big.at[block(t * U * 12, U * 12), :]
@@ -268,32 +301,7 @@
                     if last:
                         h4[(u * 3 + n) * 256 : (u * 3 + n + 1) * 256, :] = (jax.nn.silu(vals[0]) * vals[1]).astype(BF16)
 
-            @pl.when(i + NB < NK * steps)
-            def _():
-                for cp in w_load(i + NB):
-                    cp.start()
-
-            if last:
-                down(0, t)
-            else:
-                if not first:
-                    build_g(4 + k * 4 + t, 0)
-
-                @pl.when(jnp.logical_and(t == 0, k + 2 < NK))
-                def _():
-                    forward(k + 2)
-
-                @pl.when(jnp.logical_and(t == 0, k + 4 < NK))
-                def _():
-                    own(k + 4)
-
-                @pl.when(t == 2)
-                def _():
-                    diagonal(k + 1)
-
-            return carry
-
-        lax.fori_loop(0, steps, body, 0)
+        lax.fori_loop(0, steps // wide, body, 0)
 
     gather_rows(0)
     experts(0, first=True)

time: 138 us -> 136 us (0.986)
  Pallas kernels: 136 us -> 133 us
    pallas_call x1, Pallas kernels: 136 us -> 133 us  [local_layer(): pl.pallas_call(layer_kernel, out_shape=jax.ShapeDtypeStruct((rows, width)...]
where the time goes in v9:
time: 136 us; the launch traced here: 135 us
  Pallas kernels  133 us (98%)
  local copies, waits for them, and re-layouts  2.3 us (2%)
    pallas_call x1, Pallas kernels, local_layer(): pl.pallas_call(layer_kernel, out_shape=jax.ShapeDtypeStruct((rows, width)...  133 us

profile of v9, /device:TPU:0, one launch (start us, length us, event | category | flops | bytes accessed | tf_op | source)
XLA Modules:
  0.0 135.4 jit_solution(15939352096491036756)
XLA Ops:
  0.0 133.1 %moe_layer.1 = bf16[256,2048]{1,0:T(8,128)(2,1)} custom-call(s32[8,256]{1,0:T(8,128)} %bitcast.3, s32[8,256]{1,0:T(8,128)} %bitcast.4, f32[8,256]{1,0:T(8,128)} %bitcast.5, bf16[256,2048]{1,0:T(8,128)(2,1)} %tok_ref.1, bf16[16,2048,768]{2,1,0:T(8,128)(2,1)} %wg_ref.1, bf16[16,2048,768]{2,1,0:T(8,128)(2,1)} %wu_ref.1, bf16[16,768,2048]{2,1,0:T(8,128)(2,1)} %wd_ref.1), custom_call_target="tpu_custom_call" | custom-call | flops 38654705664 | bytes 150994944 | tf_op jit(solution)/shard_map/moe_layer/pallas_call | solution.py:465
  133.1 2.3 %copy.9 = bf16[256,2048]{1,0:T(8,128)(2,1)} copy(bf16[256,2048]{1,0:T(8,128)(2,1)} %moe_layer.1) | data formatting | bytes 2097152

commit v10 on v9

--- a/solution.py
+++ b/solution.py
@@ -42,9 +42,9 @@
 
 def layer_kernel(
     id_ref, slot_ref, gate_ref, tok_ref, wg_ref, wu_ref, wd_ref, out_ref,
-    rall, rt, xall, pmat, gmat, gbuf, big, wbuf, dbuf, obuf,
+    rall, rt, xall, pmat, gmat, gbuf, big, wbuf, dbuf,
     lsem, rs_sem, rr_sem, xs_sem, xr_sem, w_sem, d_sem,
-    ds_sem, dr_sem, is_sem, ir_sem, o_sem, ready,
+    ds_sem, dr_sem, is_sem, ir_sem, ready,
 ):
     data = lax.axis_index("data")
     y = lax.axis_index("node")
@@ -103,19 +103,19 @@
     rall[pl.ds(mine + 8, 8), :] = gate_ref[...]
     pl.semaphore_wait(barrier, GROUP - 1)
 
-    def r_copy(d, owner, dst):
-        ref = rall.at[pl.ds(pl.multiple_of(owner * 16, 16), 16), :]
+    def r_copy(d, half, owner, dst):
+        ref = rall.at[pl.ds(pl.multiple_of(owner * 16 + half * 8, 8), 8), :]
         return pltpu.make_async_remote_copy(
             src_ref=ref,
             dst_ref=ref,
-            send_sem=rs_sem.at[d - 1],
-            recv_sem=rr_sem.at[d - 1],
+            send_sem=rs_sem.at[half, d - 1],
+            recv_sem=rr_sem.at[half, d - 1],
             device_id=(data, dst // 4, dst % 4),
             device_id_type=MESH,
         )
 
     for d in range(1, GROUP):
-        r_copy(d, g, (g + d) % GROUP).start()
+        r_copy(d, 0, g, (g + d) % GROUP).start()
 
     def x_copy(i, k, s, dev, lo=0, n=ROWS):
         ref = xall.at[pl.ds(pl.multiple_of((k * GROUP + s) * ROWS + lo, 128), n), :]
@@ -174,10 +174,11 @@
 
     own(0)
     own(1)
-
     for d in range(1, GROUP):
-        r_copy(d, (g + GROUP - d) % GROUP, g).wait_recv()
-    rt[...] = jnp.transpose(rall[...])
+        r_copy(d, 1, g, (g + d) % GROUP).start()
+
+    for d in range(1, GROUP):
+        r_copy(d, 0, (g + GROUP - d) % GROUP, g).wait_recv()
 
     base = (g * SLOTS).astype(F32)
     ybuf = pmat
@@ -213,6 +214,9 @@
     lax.fori_loop(0, GROUP * SLOTS // PB, build_p, 0)
     forward(0)
     own(2)
+    for d in range(1, GROUP):
+        r_copy(d, 1, (g + GROUP - d) % GROUP, g).wait_recv()
+    rt[...] = jnp.transpose(rall[...])
     gn = GROUP * ROWS // GB
     lax.fori_loop(0, gn // 4, build_g, 0)
     forward(1)
@@ -417,26 +421,19 @@
 
     lax.fori_loop(NC - LAG, NC, tail, 0)
 
-    def out_copy(c):
-        cols = pl.ds(pl.multiple_of(c * CC, CC), CC)
-        return pltpu.make_async_copy(obuf.at[c], out_ref.at[:, cols], o_sem.at[c])
-
     def final(c, carry):
         ici(2, c).wait_recv()
         a = big[block(OWN + c * 8), :] + big[block(RA1 + c * 2), :] + big[block(RA2 + c), :]
         ici(3, c).wait_recv()
         b = big[block(OWN + c * 8 + 4), :] + big[block(RB1 + c * 2), :] + big[block(RB2 + c), :]
-        obuf[c, :, 0:128] = a.astype(BF16)
-        obuf[c, :, 128:256] = b.astype(BF16)
-        out_copy(c).start()
+        out_ref[:, pl.ds(pl.multiple_of(c * CC, CC), 128)] = a.astype(BF16)
+        out_ref[:, pl.ds(pl.multiple_of(c * CC + 128, 128), 128)] = b.astype(BF16)
         for i in range(4):
             ici(i, c).wait_send()
         return carry
 
     lax.fori_loop(0, NC, final, 0)
 
-    for c in range(NC):
-        out_copy(c).wait()
     for c in (NC - 2, NC - 1):
         for i in range(4):
             d2d(i, c).wait_send()
@@ -444,7 +441,8 @@
         for i in range(8):
             send(i, k).wait_send()
     for d in range(1, GROUP):
-        r_copy(d, g, (g + d) % GROUP).wait_send()
+        for half in range(2):
+            r_copy(d, half, g, (g + d) % GROUP).wait_send()
 
 
 def solution(mesh):
@@ -464,9 +462,9 @@
         dma = pltpu.SemaphoreType.DMA
         return pl.pallas_call(
             layer_kernel,
-            out_shape=jax.ShapeDtypeStruct((rows, width), BF16),
+            out_shape=pltpu.VMEM((rows, width), BF16),
             in_specs=[vmem, vmem, vmem, hbm, hbm, hbm, hbm],
-            out_specs=hbm,
+            out_specs=vmem,
             scratch_shapes=[
                 pltpu.VMEM((GROUP * 16, ROWS), F32),
                 pltpu.VMEM((ROWS, GROUP * 16), F32),
@@ -477,10 +475,9 @@
                 pltpu.VMEM((NBLK * 256, 128), F32),
                 pltpu.VMEM((NB, 2, U, KC, FF), BF16),
                 pltpu.VMEM((NBD, U, FF, CC), BF16),
-                pltpu.VMEM((NC, ROWS, CC), BF16),
                 dma((NK,)),
-                dma((GROUP - 1,)),
-                dma((GROUP - 1,)),
+                dma((2, GROUP - 1)),
+                dma((2, GROUP - 1)),
                 dma((8, NK)),
                 dma((8, NK)),
                 dma((NB, 2)),
@@ -489,11 +486,10 @@
                 dma((4, NC)),
                 dma((4, NC)),
                 dma((4, NC)),
-                dma((NC,)),
                 pltpu.SemaphoreType.REGULAR,
             ],
             compiler_params=pltpu.CompilerParams(
-                collective_id=0, has_side_effects=True, vmem_limit_bytes=67043328,
+                collective_id=0, has_side_effects=True, vmem_limit_bytes=65900000,
             ),
             cost_estimate=pl.CostEstimate(
                 flops=6 * LOCAL * GROUP * CAP * WIDTH * FF,

time: 136 us -> 135 us (level)
  no operation moved by 1% of the time
where the time goes in v10:
time: 135 us
  Pallas kernels  134 us (99%)
    pallas_call x1, Pallas kernels, local_layer(): pl.pallas_call(layer_kernel, out_shape=pltpu.VMEM((rows, width), BF16), i...  134 us

profile of v10, /device:TPU:0, one launch (start us, length us, event | category | flops | bytes accessed | tf_op | source)
XLA Modules:
  0.0 135.1 jit_solution(10340073102953842986)
XLA Ops:
  0.0 134.1 %moe_layer.1 = bf16[256,2048]{1,0:T(8,128)(2,1)S(1)} custom-call(s32[8,256]{1,0:T(8,128)} %bitcast.3, s32[8,256]{1,0:T(8,128)} %bitcast.4, f32[8,256]{1,0:T(8,128)} %bitcast.5, bf16[256,2048]{1,0:T(8,128)(2,1)} %tok_ref.1, bf16[16,2048,768]{2,1,0:T(8,128)(2,1)} %wg_ref.1, bf16[16,2048,768]{2,1,0:T(8,128)(2,1)} %wu_ref.1, bf16[16,768,2048]{2,1,0:T(8,128)(2,1)} %wd_ref.1), custom_call_target="tpu_custom_call" | custom-call | flops 38654705664 | bytes 150994944 | tf_op jit(solution)/shard_map/moe_layer/pallas_call | solution.py:463
  134.1 1.0 copy.9

commit v11 on v10

--- a/solution.py
+++ b/solution.py
@@ -214,14 +214,12 @@
     lax.fori_loop(0, GROUP * SLOTS // PB, build_p, 0)
     forward(0)
     own(2)
+    forward(1)
+    own(3)
+    diagonal(0)
     for d in range(1, GROUP):
         r_copy(d, 1, (g + GROUP - d) % GROUP, g).wait_recv()
     rt[...] = jnp.transpose(rall[...])
-    gn = GROUP * ROWS // GB
-    lax.fori_loop(0, gn // 4, build_g, 0)
-    forward(1)
-    own(3)
-    diagonal(0)
     finish(0)
 
     def gather_rows(k):
@@ -267,9 +265,9 @@
             if last:
                 down(0, tt)
             else:
-                if not first:
-                    for w in range(wide):
-                        build_g(4 + k * 4 + tt * wide + w, 0)
+                each = 4 if first else 2
+                for w in range(each):
+                    build_g((0 if first else 4 + k * 4) + tt * each + w, 0)
 
                 @pl.when(jnp.logical_and(tt == 0, k + 2 < NK))
                 def _():

time: 135 us -> 134 us (level)
    pallas_call x1, Pallas kernels: 134 us -> 133 us  [local_layer(): pl.pallas_call(layer_kernel, out_shape=pltpu.VMEM((rows, width), BF16), i...]
where the time goes in v11:
time: 134 us
  Pallas kernels  133 us (99%)
    pallas_call x1, Pallas kernels, local_layer(): pl.pallas_call(layer_kernel, out_shape=pltpu.VMEM((rows, width), BF16), i...  133 us

profile of v11, /device:TPU:0, one launch (start us, length us, event | category | flops | bytes accessed | tf_op | source)
XLA Modules:
  0.0 133.6 jit_solution(6225746808454037327)
XLA Ops:
  0.0 132.6 %moe_layer.1 = bf16[256,2048]{1,0:T(8,128)(2,1)S(1)} custom-call(s32[8,256]{1,0:T(8,128)} %bitcast.3, s32[8,256]{1,0:T(8,128)} %bitcast.4, f32[8,256]{1,0:T(8,128)} %bitcast.5, bf16[256,2048]{1,0:T(8,128)(2,1)} %tok_ref.1, bf16[16,2048,768]{2,1,0:T(8,128)(2,1)} %wg_ref.1, bf16[16,2048,768]{2,1,0:T(8,128)(2,1)} %wu_ref.1, bf16[16,768,2048]{2,1,0:T(8,128)(2,1)} %wd_ref.1), custom_call_target="tpu_custom_call" | custom-call | flops 38654705664 | bytes 150994944 | tf_op jit(solution)/shard_map/moe_layer/pallas_call | solution.py:461
  132.7 1.0 copy.9

commit v12 on v11

--- a/solution.py
+++ b/solution.py
@@ -269,13 +269,12 @@
                 for w in range(each):
                     build_g((0 if first else 4 + k * 4) + tt * each + w, 0)
 
-                @pl.when(jnp.logical_and(tt == 0, k + 2 < NK))
-                def _():
-                    forward(k + 2)
-
-                @pl.when(jnp.logical_and(tt == 0, k + 4 < NK))
-                def _():
-                    own(k + 4)
+                if first:
+
+                    @pl.when(tt == 0)
+                    def _():
+                        forward(k + 2)
+                        own(k + 4)
 
                 @pl.when(tt == 0)
                 def _():
@@ -311,6 +310,15 @@
 
     def middle(k, carry):
         gather_rows(k)
+
+        @pl.when(k + 2 < NK)
+        def _():
+            forward(k + 2)
+
+        @pl.when(k + 4 < NK)
+        def _():
+            own(k + 4)
+
         experts(k)
 
         finish(k + 1)

time: 134 us -> 134 us (level)
  no operation moved by 1% of the time
where the time goes in v12:
time: 134 us
  Pallas kernels  133 us (99%)
    pallas_call x1, Pallas kernels, local_layer(): pl.pallas_call(layer_kernel, out_shape=pltpu.VMEM((rows, width), BF16), i...  133 us

profile of v12, /device:TPU:0, one launch (start us, length us, event | category | flops | bytes accessed | tf_op | source)
XLA Modules:
  0.0 133.5 jit_solution(9778664942589345351)
XLA Ops:
  0.0 132.5 %moe_layer.1 = bf16[256,2048]{1,0:T(8,128)(2,1)S(1)} custom-call(s32[8,256]{1,0:T(8,128)} %bitcast.3, s32[8,256]{1,0:T(8,128)} %bitcast.4, f32[8,256]{1,0:T(8,128)} %bitcast.5, bf16[256,2048]{1,0:T(8,128)(2,1)} %tok_ref.1, bf16[16,2048,768]{2,1,0:T(8,128)(2,1)} %wg_ref.1, bf16[16,2048,768]{2,1,0:T(8,128)(2,1)} %wu_ref.1, bf16[16,768,2048]{2,1,0:T(8,128)(2,1)} %wd_ref.1), custom_call_target="tpu_custom_call" | custom-call | flops 38654705664 | bytes 150994944 | tf_op jit(solution)/shard_map/moe_layer/pallas_call | solution.py:469
  132.5 1.0 copy.9
